TPU v7x, 32 devices: a whole 2x2x4 slice. The times are simulated.
32 devices in a mesh: pop: 16 (over z, x, core), hid: 2 (over y).
Axes of the slice: x: 2, y: 2, z: 4, core: 2. Of those that a mesh axis runs over, the one named last changes fastest.
Arguments:
- tokens: bfloat16 [512, 4096], P('pop', 'hid'), may hold values from -6 to 6
- fitness_ranks: int32 [32], replicated, may hold values from 0 to 31, each once
- gate_weight: bfloat16 [4096, 16384], P('hid', 'pop'), may hold values from -0.09375 to 0.09375
- up_weight: bfloat16 [4096, 16384], P('hid', 'pop'), may hold values from -0.09375 to 0.09375
- down_weight: bfloat16 [16384, 4096], P('pop', 'hid'), may hold values from -0.046875 to 0.046875
- gate_input_factor: bfloat16 [32, 4, 4096], P(None, None, 'hid'), may hold values from -6 to 6
- up_input_factor: bfloat16 [32, 4, 4096], P(None, None, 'hid'), may hold values from -6 to 6
- down_right: bfloat16 [32, 4, 4096], P(None, None, 'hid'), may hold values from -6 to 6
- gate_output_factor: bfloat16 [32, 4, 16384], P('pop'), may hold values from -6 to 6
- up_output_factor: bfloat16 [32, 4, 16384], P('pop'), may hold values from -6 to 6
- down_left: bfloat16 [32, 4, 16384], P('pop'), may hold values from -6 to 6
Outputs:
- mixed: bfloat16 [512, 4096], P('pop', 'hid')
- gate_step: float32 [4096, 16384], P('hid', 'pop')
- up_step: float32 [4096, 16384], P('hid', 'pop')
- down_step: float32 [16384, 4096], P('pop', 'hid')
Inputs may be any that keep to these rules, and one draw needn't show every extreme that they name: `fitness_ranks`: every rank appears exactly once.
All inputs are finite; a program needn't handle non-finite values.
Results may differ from a plain program's by a relative error of at most 0.025.
Values may be sent and summed in bfloat16 or wider, within the bound.
No kernel may reach another device: no remote copies, remote signals or barrier semaphores. Data moves between devices by JAX's collectives and lax.ppermute only.
A program may use at most 128 MiB of HBM per device.

v0:
```python
import functools
import math

import jax
import jax.numpy as jnp
from jax import lax
from jax.experimental import pallas as pl
from jax.experimental.pallas import tpu as pltpu
from jax.sharding import PartitionSpec as P


MODEL_WIDTH = 4096
HIDDEN_UNITS = 16384
RANK = 4
SAMPLE_LENGTH = 16
X_COUNT = 2
CORE_COUNT = 2
PLANE = X_COUNT * CORE_COUNT
LANES = 128
F32 = jnp.float32
BF16 = jnp.bfloat16


def dot(a, b):
    return jnp.dot(a, b, preferred_element_type=F32)


def dot_nt(a, b):
    return lax.dot_general(a, b, (((1,), (1,)), ((), ())), preferred_element_type=F32)


def split_high_low(v):
    high = v.astype(BF16)
    return high, (v - high.astype(F32)).astype(BF16)


def place():
    p = lax.axis_index("pop")
    y = lax.axis_index("hid")
    return p // PLANE, (p // CORE_COUNT) % X_COUNT, p % CORE_COUNT, y


def iota(shape, dim):
    return lax.broadcasted_iota(jnp.int32, shape, dim)


def row_members(shape, members):
    unit = iota(shape, 0) // SAMPLE_LENGTH
    out = jnp.zeros(shape, jnp.int32)
    for index, member in enumerate(members):
        out = jnp.where(unit == index, member, out)
    return out


def compiler_params(limit_mib):
    return pltpu.CompilerParams(vmem_limit_bytes=limit_mib * 1024 * 1024)


IN_VMEM = pl.BlockSpec(memory_space=pltpu.VMEM)
IN_HBM = pl.BlockSpec(memory_space=pltpu.HBM)
IN_SMEM = pl.BlockSpec(memory_space=pltpu.SMEM)


def fixed(*arrays):
    return [pltpu.with_memory_space_constraint(v, pltpu.HBM) for v in arrays]


def fetch(pairs, sem):
    copies = [pltpu.make_async_copy(a, b, sem.at[i]) for i, (a, b) in enumerate(pairs)]
    for copy in copies:
        copy.start()
    return copies


def pack_kernel(z_count, gate_in, up_in, down_in, *refs):
    outs, parts, sem = refs[:PLANE], refs[PLANE : PLANE + 3], refs[PLANE + 3]
    for copy in fetch(zip((gate_in, up_in, down_in), parts), sem):
        copy.wait()
    z, x, c, _ = place()
    mem = parts[0].shape[0]
    part = outs[0].shape[2]
    for q in range(PLANE):
        xs, cs = jnp.bitwise_xor(x, q % X_COUNT), jnp.bitwise_xor(c, q // X_COUNT)
        for k in range(z_count):
            to = (lax.rem(z + k, z_count) * X_COUNT + xs) * CORE_COUNT + cs
            at = pl.ds(pl.multiple_of(to * part, LANES), part)
            rows = [ref[m, :, at].astype(F32) for ref in parts for m in range(mem)]
            outs[q][k] = jnp.concatenate(rows, axis=0).astype(BF16)


def pack(gate, up, down, z_count):
    mem, rank, hidden = gate.shape
    part = hidden // (z_count * PLANE)
    return pl.pallas_call(
        functools.partial(pack_kernel, z_count),
        in_specs=[IN_HBM] * 3,
        out_specs=[IN_VMEM] * PLANE,
        out_shape=[jax.ShapeDtypeStruct((z_count, 3 * mem * rank, part), BF16)] * PLANE,
        scratch_shapes=[pltpu.VMEM(gate.shape, BF16)] * 3 + [pltpu.SemaphoreType.DMA((3,))],
        compiler_params=compiler_params(8),
        cost_estimate=pl.CostEstimate(
            flops=512 * gate.size, bytes_accessed=12 * gate.size, transcendentals=0
        ),
        name="pack",
    )(*fixed(gate, up, down))


def merge_kernel(*refs):
    ins, outs, rows_ref = refs[:PLANE], refs[PLANE:-1], refs[-1]
    _, x, c, _ = place()
    group = ins[0].shape[1] // 3
    tall = 2 * group
    for k, out in enumerate(outs):
        for q in range(PLANE):
            xs, cs = jnp.bitwise_xor(x, q % X_COUNT), jnp.bitwise_xor(c, q // X_COUNT)
            slot = xs * CORE_COUNT + cs
            out[pl.ds(pl.multiple_of(slot * tall, tall), tall), :] = ins[q][k, :tall, :]
            rows_ref[pl.ds(pl.multiple_of(slot * group, group), group), :] = ins[q][
                k, tall:, :
            ].astype(F32)
        out[PLANE * tall :, :] = rows_ref[...].astype(BF16)


def merge(blocks):
    z_count, rows, part = blocks[0].shape
    return pl.pallas_call(
        merge_kernel,
        in_specs=[IN_VMEM] * PLANE,
        out_specs=[IN_VMEM] * z_count,
        out_shape=[jax.ShapeDtypeStruct((PLANE * rows, part), BF16)] * z_count,
        scratch_shapes=[pltpu.VMEM((PLANE * rows // 3, part), F32)],
        compiler_params=compiler_params(8),
        cost_estimate=pl.CostEstimate(
            flops=512 * z_count * rows * part, bytes_accessed=16 * rows * part, transcendentals=0
        ),
        name="merge",
    )(*blocks)


def load_kernel(mem, gif_in, uif_in, gw_in, uw_in, giu_ref, gw_ref, uw_ref, gif_ref, uif_ref, sem):
    copies = fetch(
        ((gif_in, gif_ref), (uif_in, uif_ref), (gw_in, gw_ref), (uw_in, uw_ref)), sem
    )
    for copy in copies[:2]:
        copy.wait()
    tall = 2 * mem * RANK
    for p in range(gif_ref.shape[0] // mem):
        rows = [ref[p * mem + m].astype(F32) for ref in (gif_ref, uif_ref) for m in range(mem)]
        giu_ref[p * tall : (p + 1) * tall] = jnp.concatenate(rows, axis=0).astype(BF16)
    for copy in copies[2:]:
        copy.wait()


def load(gif, uif, gw, uw, mem):
    members, rank, width = gif.shape
    return pl.pallas_call(
        functools.partial(load_kernel, mem),
        in_specs=[IN_HBM] * 4,
        out_specs=[IN_VMEM] * 3,
        out_shape=[
            pltpu.VMEM((2 * members * rank, width), BF16),
            pltpu.VMEM(gw.shape, BF16),
            pltpu.VMEM(uw.shape, BF16),
        ],
        scratch_shapes=[pltpu.VMEM(gif.shape, BF16)] * 2 + [pltpu.SemaphoreType.DMA((4,))],
        compiler_params=compiler_params(16),
        cost_estimate=pl.CostEstimate(
            flops=1024 * gw.size, bytes_accessed=4 * gw.size, transcendentals=0
        ),
        name="load",
    )(*fixed(gif, uif, gw, uw))


def scaled(ranks_ref, members, value, first, number):
    member = iota((value.shape[0], 1), 0) // RANK % number
    rank = jnp.zeros(member.shape, jnp.int32)
    for m in range(number):
        rank = jnp.where(member == m, ranks_ref[first + m], rank)
    return (value * (rank.astype(F32) / (members - 1) - 0.5)).astype(BF16)


def turn_into(out_ref, in_ref):
    columns = min(256, in_ref.shape[1])
    for j in range(in_ref.shape[1] // columns):
        at = slice(j * columns, (j + 1) * columns)
        out_ref[at] = in_ref[:, at].T.astype(BF16)


def turn_kernel(mem, ranks_ref, gif_in, uif_in, out_ref, gif_ref, uif_ref, rows_ref, sem):
    for copy in fetch(((gif_in, gif_ref), (uif_in, uif_ref)), sem):
        copy.wait()
    members = gif_ref.shape[0]
    tall = 2 * mem * RANK
    for p in range(members // mem):
        pieces = [ref[p * mem + m].astype(F32) for ref in (gif_ref, uif_ref) for m in range(mem)]
        value = scaled(ranks_ref, members, jnp.concatenate(pieces, axis=0), p * mem, mem)
        rows_ref[p * tall : (p + 1) * tall] = value.astype(F32)
    turn_into(out_ref, rows_ref)


def turn(ranks, gif, uif, mem):
    members, rank, width = gif.shape
    lanes = 2 * members * rank
    return pl.pallas_call(
        functools.partial(turn_kernel, mem),
        in_specs=[IN_SMEM] + [IN_HBM] * 2,
        out_specs=IN_VMEM,
        out_shape=jax.ShapeDtypeStruct((width, lanes), BF16),
        scratch_shapes=[pltpu.VMEM(gif.shape, BF16)] * 2
        + [pltpu.VMEM((lanes, width), F32), pltpu.SemaphoreType.DMA((2,))],
        compiler_params=compiler_params(12),
        cost_estimate=pl.CostEstimate(
            flops=4096 * gif.size, bytes_accessed=8 * gif.size, transcendentals=0
        ),
        name="turn",
    )(ranks, *fixed(gif, uif))


def arrange_kernel(z_count, ranks_ref, right_in, dw_in, *refs):
    gots = refs[:z_count]
    gu_ref, d_ref, dt_ref, right_ref, sright_ref, dw_ref = refs[z_count : z_count + 6]
    raw_ref, rows_ref, sem = refs[z_count + 6 :]
    copies = fetch(((right_in, raw_ref), (dw_in, dw_ref)), sem)
    z, _, _, _ = place()
    third = gots[0].shape[0] // 3
    members = raw_ref.shape[0]
    for k, got in enumerate(gots):
        zs = lax.rem(z - k + z_count, z_count)
        gu_ref[pl.ds(pl.multiple_of(zs * 2 * third, 2 * third), 2 * third), :] = got[: 2 * third, :]
        down_at = pl.ds(pl.multiple_of(zs * third, third), third)
        d_ref[down_at, :] = got[2 * third :, :]
        rows_ref[down_at, :] = got[2 * third :, :].astype(F32)
    turn_into(dt_ref, rows_ref)
    copies[0].wait()
    number = 4
    tall = number * RANK
    for p in range(members // number):
        value = jnp.concatenate([raw_ref[p * number + m].astype(F32) for m in range(number)], axis=0)
        right_ref[p * tall : (p + 1) * tall] = value.astype(BF16)
        sright_ref[p * tall : (p + 1) * tall] = scaled(ranks_ref, members, value, p * number, number)
    copies[1].wait()


def arrange(ranks, gots, right, dw):
    hidden = gots[0].shape[1]
    members, rank, width = right.shape
    lanes = members * rank
    return pl.pallas_call(
        functools.partial(arrange_kernel, len(gots)),
        in_specs=[IN_SMEM] + [IN_HBM] * 2 + [IN_VMEM] * len(gots),
        out_specs=[IN_VMEM] * 6,
        out_shape=[
            pltpu.VMEM((2 * lanes, hidden), BF16),
            pltpu.VMEM((lanes, hidden), BF16),
            pltpu.VMEM((hidden, lanes), BF16),
            pltpu.VMEM((lanes, width), BF16),
            pltpu.VMEM((lanes, width), BF16),
            pltpu.VMEM(dw.shape, BF16),
        ],
        scratch_shapes=[
            pltpu.VMEM(right.shape, BF16),
            pltpu.VMEM((lanes, hidden), F32),
            pltpu.SemaphoreType.DMA((2,)),
        ],
        compiler_params=compiler_params(16),
        cost_estimate=pl.CostEstimate(
            flops=1024 * dw.size, bytes_accessed=4 * dw.size, transcendentals=0
        ),
        name="arrange",
    )(ranks, *fixed(right, dw), *gots)


def unit_members(units, per_block, shifts, z, z_count, start):
    members = []
    for w in range(units):
        unit = start(w)
        zs = jnp.int32(0)
        for b, shift in enumerate(shifts):
            zs = jnp.where(unit // per_block == b, lax.rem(z + shift, z_count), zs)
        members.append(zs * per_block + unit % per_block)
    return members


def lane_members(shape, group):
    lane = iota(shape, 1)
    return lane // (2 * group) * (group // RANK) + lane % group // RANK


def gate_up_kernel(shifts, z_count, hid_count, mem_local, *refs):
    blocks = len(shifts)
    pieces = refs[: PLANE * blocks]
    gw_ref, uw_ref, giu_ref = refs[PLANE * blocks : PLANE * blocks + 3]
    sends = refs[PLANE * blocks + 3 : PLANE * blocks + 2 + hid_count]
    keep_ref, keep_proj_ref, rows_ref = refs[PLANE * blocks + 2 + hid_count :]
    z, x, c, y = place()
    per_block = PLANE * mem_local
    units = per_block * blocks
    per_part = units // hid_count
    part_rows = per_part * SAMPLE_LENGTH
    hidden = keep_ref.shape[1] // 2
    columns = min(256, hidden)
    group = mem_local * RANK
    for b in range(blocks):
        for q in range(PLANE):
            rx, rc = q % 2, q // 2
            piece = pieces[b * PLANE + q]
            slot = b * PLANE + jnp.bitwise_xor(x, rx) * CORE_COUNT + jnp.bitwise_xor(c, rc)
            for m in range(mem_local):
                unit = slot * mem_local + m
                rel = lax.rem(unit // per_part - y - 1 + hid_count, hid_count)
                row = (rel * per_part + unit % per_part) * SAMPLE_LENGTH
                rows_ref[pl.ds(pl.multiple_of(row, SAMPLE_LENGTH), SAMPLE_LENGTH), :] = piece[
                    m * SAMPLE_LENGTH : (m + 1) * SAMPLE_LENGTH, :
                ]
    members = unit_members(
        units,
        per_block,
        shifts,
        z,
        z_count,
        lambda p: lax.rem(p // per_part + y + 1, hid_count) * per_part + p % per_part,
    )
    rows = rows_ref[...]
    projected = dot_nt(rows, giu_ref[...])
    mine = row_members(projected.shape, members) == lane_members(projected.shape, group)
    high, low = split_high_low(jnp.where(mine, projected, 0.0))
    shape = (projected.shape[1], LANES)
    lane = iota(shape, 0) % RANK + 2 * RANK * (iota(shape, 0) // group % 2)

    def pick(level):
        return (lane + RANK * level == iota(shape, 1)).astype(F32).astype(BF16)

    packed = (dot(high, pick(0)) + dot(low, pick(1))).astype(BF16)
    for s in range(hid_count - 1):
        sends[s][:, 2 * hidden :] = packed[s * part_rows : (s + 1) * part_rows]
    keep_proj_ref[...] = packed[(hid_count - 1) * part_rows :]
    for j in range(hidden // columns):
        for index, ref in enumerate((gw_ref, uw_ref)):
            value = dot(rows, ref[:, j * columns : (j + 1) * columns])
            at = slice(index * hidden + j * columns, index * hidden + (j + 1) * columns)
            for s in range(hid_count - 1):
                sends[s][:, at] = value[s * part_rows : (s + 1) * part_rows].astype(BF16)
            keep_ref[:, at] = value[(hid_count - 1) * part_rows :]


def gate_up(pieces, gw, uw, giu, shifts, z_count, hid_count):
    rows, width = pieces[0].shape
    hidden = gw.shape[1]
    total = rows * PLANE * len(shifts)
    part = total // hid_count
    send_shape = (part, 2 * hidden + LANES)
    return pl.pallas_call(
        functools.partial(
            gate_up_kernel, shifts, z_count, hid_count, rows // SAMPLE_LENGTH
        ),
        in_specs=[IN_VMEM] * (len(pieces) + 3),
        out_specs=[IN_VMEM] * (hid_count + 1),
        out_shape=[jax.ShapeDtypeStruct(send_shape, BF16)] * (hid_count - 1)
        + [
            jax.ShapeDtypeStruct((part, 2 * hidden), F32),
            jax.ShapeDtypeStruct((part, LANES), BF16),
        ],
        scratch_shapes=[pltpu.VMEM((total, width), BF16)],
        compiler_params=compiler_params(24),
        cost_estimate=pl.CostEstimate(
            flops=4 * total * width * hidden, bytes_accessed=4 * width * hidden, transcendentals=0
        ),
        name="gate_up",
    )(*pieces, gw, uw, giu)


def hidden_kernel(shifts, z_count, hid_count, mem_local, scale, *refs):
    keep_ref, keep_proj = refs[:2]
    recvs = refs[2 : 1 + hid_count]
    cols_ref, out_ref = refs[1 + hid_count :]
    z, _, _, y = place()
    per_block = PLANE * mem_local
    per_part = per_block * len(shifts) // hid_count
    lanes, hidden = cols_ref.shape
    group = mem_local * RANK
    rows = keep_proj.shape[0]
    members = unit_members(
        per_part, per_block, shifts, z, z_count, lambda w: y * per_part + w
    )
    mine = row_members((rows, lanes), members) == lane_members((rows, lanes), group)
    source, target = iota((LANES, lanes), 0), iota((LANES, lanes), 1)
    base = target % RANK + 2 * RANK * (target // group % 2)
    spread = ((source == base) | (source == base + RANK)).astype(F32).astype(BF16)
    value = dot(keep_proj[...], spread)
    for ref in recvs:
        value = value + dot(ref[:, 2 * hidden :], spread)
    value = jnp.where(mine, value, 0.0) * scale
    of_gate = iota((rows, lanes), 1) // group % 2 == 0
    gate_high, gate_low = split_high_low(jnp.where(of_gate, value, 0.0))
    up_high, up_low = split_high_low(jnp.where(of_gate, 0.0, value))
    stack = jnp.concatenate([gate_high, gate_low, up_high, up_low], axis=0)
    columns = min(256, hidden)
    for j in range(hidden // columns):
        lowrank = dot(stack, cols_ref[:, j * columns : (j + 1) * columns])

        def total(index):
            at = slice(index * hidden + j * columns, index * hidden + (j + 1) * columns)
            value = keep_ref[:, at]
            for ref in recvs:
                value = value + ref[:, at].astype(F32)
            first = 2 * index * rows
            return value + (lowrank[first : first + rows] + lowrank[first + rows : first + 2 * rows])

        gate, up = total(0), total(1)
        out_ref[:, j * columns : (j + 1) * columns] = (
            gate / (1.0 + jnp.exp(-gate)) * up
        ).astype(BF16)


def make_hidden(keep, keep_proj, recvs, cols, shifts, z_count, hid_count, mem_local, scale):
    part = keep.shape[0]
    hidden = keep.shape[1] // 2
    lanes = cols.shape[0]
    return pl.pallas_call(
        functools.partial(hidden_kernel, shifts, z_count, hid_count, mem_local, scale),
        in_specs=[IN_VMEM] * (3 + len(recvs)),
        out_specs=IN_VMEM,
        out_shape=jax.ShapeDtypeStruct((part, hidden), BF16),
        compiler_params=compiler_params(12),
        cost_estimate=pl.CostEstimate(
            flops=8 * part * lanes * hidden, bytes_accessed=8 * part * hidden, transcendentals=0
        ),
        name="make_hidden",
    )(keep, keep_proj, *recvs, cols)


def down_kernel(shifts, z_count, hid_count, mem_local, scale, *refs):
    blocks = len(shifts)
    parts = refs[:hid_count]
    dw_ref, cols_ref, right_ref, send_ref, keep_ref, rows_ref = refs[hid_count:]
    z, x, c, y = place()
    units = PLANE * mem_local * blocks
    per_part = units // hid_count
    half, width = send_ref.shape
    for s in range(hid_count):
        for w in range(per_part):
            unit = lax.rem(y + s, hid_count) * per_part + w
            b = unit // (PLANE * mem_local)
            rx = jnp.bitwise_xor(unit // (CORE_COUNT * mem_local) % X_COUNT, x)
            rc = jnp.bitwise_xor(unit // mem_local % CORE_COUNT, c)
            slot = ((1 - rc) * X_COUNT + 1 - rx) * blocks + b
            row = (slot * mem_local + unit % mem_local) * SAMPLE_LENGTH
            rows_ref[pl.ds(pl.multiple_of(row, SAMPLE_LENGTH), SAMPLE_LENGTH), :] = parts[s][
                w * SAMPLE_LENGTH : (w + 1) * SAMPLE_LENGTH, :
            ]
    members = []
    for p in range(units):
        slot, m = p // mem_local, p % mem_local
        q, b = slot // blocks, slot % blocks
        xs = jnp.bitwise_xor(x, 1 - q % X_COUNT)
        cs = jnp.bitwise_xor(c, 1 - q // X_COUNT)
        zs = lax.rem(z + shifts[b], z_count)
        members.append(((zs * X_COUNT + xs) * CORE_COUNT + cs) * mem_local + m)
    rows = rows_ref[...]
    projected = dot_nt(rows, cols_ref[...])
    mine = row_members(projected.shape, members) == iota(projected.shape, 1) // RANK
    both = jnp.concatenate(split_high_low(jnp.where(mine, projected, 0.0) * scale), axis=1)
    columns = min(256, width)
    for j in range(width // columns):
        at = slice(j * columns, (j + 1) * columns)
        right = right_ref[:, at]
        value = dot(rows, dw_ref[:, at]) + dot(both, jnp.concatenate([right, right], axis=0))
        send_ref[:, at] = value[:half].astype(BF16)
        keep_ref[:, at] = value[half:]


def down(parts, dw, cols, right, shifts, z_count, hid_count, mem_local, scale):
    part, hidden = parts[0].shape
    width = dw.shape[1]
    total = part * hid_count
    return pl.pallas_call(
        functools.partial(down_kernel, shifts, z_count, hid_count, mem_local, scale),
        in_specs=[IN_VMEM] * (hid_count + 3),
        out_specs=[IN_VMEM] * 2,
        out_shape=[
            jax.ShapeDtypeStruct((total // 2, width), BF16),
            jax.ShapeDtypeStruct((total // 2, width), F32),
        ],
        scratch_shapes=[pltpu.VMEM((total, hidden), BF16)],
        compiler_params=compiler_params(16),
        cost_estimate=pl.CostEstimate(
            flops=2 * total * width * hidden, bytes_accessed=2 * width * hidden, transcendentals=0
        ),
        name="down",
    )(*parts, dw, cols, right)


def input_step_kernel(index, group, factor, in_ref, cols_ref, out_ref):
    rows = out_ref.shape[0]
    left = in_ref[pl.ds(pl.multiple_of(pl.program_id(0) * rows, LANES), rows), :]
    belongs = iota(left.shape, 1) // group % 2 == index
    left = jnp.where(belongs, left.astype(F32), 0.0).astype(BF16)
    out_ref[...] = factor * dot(left, cols_ref[...])


def input_step(index, group, factor, in_factor, cols):
    width, lanes = in_factor.shape
    hidden = cols.shape[1]
    rows = min(512, width)
    return pl.pallas_call(
        functools.partial(input_step_kernel, index, group, factor),
        grid=(width // rows,),
        in_specs=[IN_VMEM] * 2,
        out_specs=pl.BlockSpec((rows, hidden), lambda i: (i, 0)),
        out_shape=jax.ShapeDtypeStruct((width, hidden), F32),
        compiler_params=compiler_params(12),
        cost_estimate=pl.CostEstimate(
            flops=8 * width * lanes * hidden, bytes_accessed=4 * width * hidden, transcendentals=0
        ),
    )(in_factor, cols)


def down_step_kernel(factor, left_ref, right_ref, out_ref):
    rows = out_ref.shape[0]
    left = left_ref[pl.ds(pl.multiple_of(pl.program_id(0) * rows, LANES), rows), :]
    out_ref[...] = factor * dot(left, right_ref[...])


def down_step(factor, left, right):
    hidden, lanes = left.shape
    width = right.shape[1]
    rows = min(256, hidden)
    return pl.pallas_call(
        functools.partial(down_step_kernel, factor),
        grid=(hidden // rows,),
        in_specs=[IN_VMEM] * 2,
        out_specs=pl.BlockSpec((rows, width), lambda i: (i, 0)),
        out_shape=jax.ShapeDtypeStruct((hidden, width), F32),
        compiler_params=compiler_params(12),
        cost_estimate=pl.CostEstimate(
            flops=8 * width * lanes * hidden, bytes_accessed=4 * width * hidden, transcendentals=0
        ),
        name="down_step",
    )(left, right)


def local(
    tokens,
    fitness_ranks,
    gate_weight,
    up_weight,
    down_weight,
    gate_input_factor,
    up_input_factor,
    down_right,
    gate_output_factor,
    up_output_factor,
    down_left,
):
    pop_count = lax.axis_size("pop")
    hid_count = lax.axis_size("hid")
    z_count = pop_count // PLANE
    tok_local, _ = tokens.shape
    mem_local = tok_local // SAMPLE_LENGTH
    members = mem_local * pop_count
    scale_in = 0.5 / math.sqrt(MODEL_WIDTH * RANK)
    scale_out = 0.5 / math.sqrt(HIDDEN_UNITS * RANK)
    factor = 1.0 / math.sqrt(members * RANK)

    everyone = range(pop_count)
    core_pairs = [(i, i ^ 1) for i in everyone]
    x_pairs = [(i, i ^ CORE_COUNT) for i in everyone]

    def forward(k):
        return [(i, (i + k * PLANE) % pop_count) for i in everyone]

    def along(v, pairs):
        return lax.ppermute(v, "pop", pairs)

    groups = GROUPS(z_count)

    blocks = {}
    for k in range(z_count):
        own = tokens if k == 0 else along(tokens, forward(z_count - k))
        from_x = along(own, x_pairs)
        from_core = along(own, core_pairs)
        from_both = along(from_x, core_pairs)
        blocks[k] = [own, from_x, from_core, from_both]

    near, near_x, far, far_x = pack(gate_output_factor, up_output_factor, down_left, z_count)
    from_x = along(near_x, x_pairs)
    far_x = along(far_x, core_pairs)
    far = along(far, core_pairs)
    far_x = along(far_x, x_pairs)
    joined = merge([near, from_x, far, far_x])
    gots = []
    for k in range(z_count):
        gots.append(along(joined[k], forward(k)) if k else joined[k])
    giu, gate_v, up_v = load(gate_input_factor, up_input_factor, gate_weight, up_weight, mem_local)
    scaled_giu = turn(fitness_ranks, gate_input_factor, up_input_factor, mem_local)
    gu_cols, d_cols, d_turned, right, scaled_right, down_v = arrange(
        fitness_ranks, gots, down_right, down_weight
    )

    total = None
    for shifts in groups:
        pieces = [piece for k in shifts for piece in blocks[k]]
        *sends, keep, keep_proj = gate_up(
            pieces, gate_v, up_v, giu, shifts, z_count, hid_count
        )
        recvs = [
            lax.ppermute(v, "hid", [(i, (i + s + 1) % hid_count) for i in range(hid_count)])
            for s, v in enumerate(sends)
        ]
        mine = make_hidden(
            keep, keep_proj, recvs, gu_cols, shifts, z_count, hid_count, mem_local, scale_in
        )
        parts = [mine] + [
            lax.ppermute(mine, "hid", [((i + s) % hid_count, i) for i in range(hid_count)])
            for s in range(1, hid_count)
        ]
        send, held = down(
            parts, down_v, d_cols, right, shifts, z_count, hid_count, mem_local, scale_out
        )
        held = held + along(send, core_pairs).astype(F32)
        half = held.shape[0] // 2
        held = held[half:] + along(held[:half].astype(BF16), x_pairs).astype(F32)
        for b, k in enumerate(shifts):
            piece = held[b * tok_local : (b + 1) * tok_local]
            if k:
                piece = along(piece.astype(BF16), forward(k)).astype(F32)
            total = piece if total is None else total + piece
    mixed = total.astype(BF16)

    group = mem_local * RANK
    gate_step = input_step(0, group, factor, scaled_giu, gu_cols)
    up_step = input_step(1, group, factor, scaled_giu, gu_cols)
    step = down_step(factor, d_turned, scaled_right)
    return (mixed, gate_step, up_step, step)


def GROUPS(z_count):
    return [(1,), *[tuple(range(z_count))[i : i + 2] for i in range(2, z_count, 2)], (0,)]


def solution(mesh):
    in_specs = (
        P("pop", "hid"),
        P(),
        P("hid", "pop"),
        P("hid", "pop"),
        P("pop", "hid"),
        P(None, None, "hid"),
        P(None, None, "hid"),
        P(None, None, "hid"),
        P("pop", None, None),
        P("pop", None, None),
        P("pop", None, None),
    )
    out_specs = (P("pop", "hid"), P("hid", "pop"), P("hid", "pop"), P("pop", "hid"))
    return jax.shard_map(local, mesh=mesh, in_specs=in_specs, out_specs=out_specs, check_vma=False)
```

profile of v0, /device:TPU:0, one launch (start us, length us, event | category | flops | bytes accessed | tf_op | source)
XLA Modules:
  0.0 116.5 jit_solution(3920944475091346166)
XLA Ops:
  0.6 3.0 %collective-permute-start.30 = (bf16[32,2048]{1,0:T(8,128)(2,1)}, bf16[32,2048]{1,0:T(8,128)(2,1)S(1)}, u32[]{:S(2)}, u32[]{:S(2)}) collective-permute-start(bf16[32,2048]{1,0:T(8,128)(2,1)} %refs_0_.1), channel_id=1, source_target_pairs={{0,4},{2,6},{4,0},{6,2},{8,12},{10,14},{12,8},{14,10},{16,20},{18,... | collective-permute-start | bytes 393224 | tf_op jit(solution)/shard_map/ppermute | solution.py:573
  3.7 1.3 %pack.1 = (bf16[4,24,1024]{2,1,0:T(8,128)(2,1)S(1)}, bf16[4,24,1024]{2,1,0:T(8,128)(2,1)S(1)}, bf16[4,24,1024]{2,1,0:T(8,128)(2,1)S(1)}, bf16[4,24,1024]{2,1,0:T(8,128)(2,1)S(1)}) custom-call(bf16[2,4,16384]{2,1,0:T(4,128)(2,1)} %gate_in.1, bf16[2,4,16384]{2,1,0:T(4,128)(2,1)} %up_in.1, bf16[2,4,16384]{2,1,0:T(4,128)(2,1)} %down_in.1), custom_call_target="tpu_custom_call" | custom-call | flops 67108864 | bytes 1572864 | tf_op jit(solution)/shard_map/pack/pallas_call | solution.py:94
  5.1 0.5 collective-permute-start.7
  5.6 2.8 %collective-permute-start.16 = (bf16[32,2048]{1,0:T(8,128)(2,1)}, bf16[32,2048]{1,0:T(8,128)(2,1)S(1)}, u32[]{:S(2)}, u32[]{:S(2)}) collective-permute-start(bf16[32,2048]{1,0:T(8,128)(2,1)} %refs_0_.1), channel_id=1, source_target_pairs={{0,16},{2,18},{4,20},{6,22},{8,24},{10,26},{12,28},{14,30},{16,0},... | collective-permute-start | bytes 393224 | tf_op jit(solution)/shard_map/ppermute | solution.py:573
  8.4 1.6 %collective-permute-start.20 = (bf16[32,2048]{1,0:T(8,128)(2,1)}, bf16[32,2048]{1,0:T(8,128)(2,1)S(1)}, u32[]{:S(2)}, u32[]{:S(2)}) collective-permute-start(bf16[32,2048]{1,0:T(8,128)(2,1)} %refs_0_.1), channel_id=1, source_target_pairs={{0,8},{2,10},{4,12},{6,14},{8,16},{10,18},{12,20},{14,22},{16,24},... | collective-permute-start | bytes 393224 | tf_op jit(solution)/shard_map/ppermute | solution.py:573
  10.0 2.2 %collective-permute-start = (bf16[32,2048]{1,0:T(8,128)(2,1)}, bf16[32,2048]{1,0:T(8,128)(2,1)S(1)}, u32[]{:S(2)}, u32[]{:S(2)}) collective-permute-start(bf16[32,2048]{1,0:T(8,128)(2,1)} %refs_0_.1), channel_id=1, source_target_pairs={{0,24},{2,26},{4,28},{6,30},{8,0},{10,2},{12,4},{14,6},{16,8},{18,... | collective-permute-start | bytes 393224 | tf_op jit(solution)/shard_map/ppermute | solution.py:573
  12.2 6.5 %collective-permute-done.16.refs_0_ = bf16[32,2048]{1,0:T(8,128)(2,1)S(1)} collective-permute-done((bf16[32,2048]{1,0:T(8,128)(2,1)}, bf16[32,2048]{1,0:T(8,128)(2,1)S(1)}, u32[]{:S(2)}, u32[]{:S(2)}) %collective-permute-start.16) | collective-permute-done | bytes 131104 | tf_op jit(solution)/shard_map/ppermute | solution.py:573
  18.8 0.5 collective-permute-start.32
  19.8 1.5 %collective-permute-start.17 = (bf16[32,2048]{1,0:T(8,128)(2,1)S(1)}, bf16[32,2048]{1,0:T(8,128)(2,1)S(1)}, u32[]{:S(2)}, u32[]{:S(2)}) collective-permute-start(bf16[32,2048]{1,0:T(8,128)(2,1)S(1)} %collective-permute-done.16.refs_0_), channel_id=1, source_target_pairs={{0,4},{2,6},{4,0},{6,2},{8,12},{10,14},{12,8},{14,10},{16,20},{18,... | collective-permute-start | bytes 393224 | tf_op jit(solution)/shard_map/ppermute | solution.py:573
  21.8 1.5 %collective-permute-start.8 = (bf16[4,24,1024]{2,1,0:T(8,128)(2,1)S(1)}, bf16[4,24,1024]{2,1,0:T(8,128)(2,1)S(1)}, u32[]{:S(2)}, u32[]{:S(2)}) collective-permute-start(bf16[4,24,1024]{2,1,0:T(8,128)(2,1)S(1)} %collective-permute-done.7), channel_id=1, source_target_pairs={{0,4},{2,6},{4,0},{6,2},{8,12},{10,14},{12,8},{14,10},{16,20},{18,... | collective-permute-start | bytes 589832 | tf_op jit(solution)/shard_map/ppermute | solution.py:573
  23.4 3.8 %load.1 = (bf16[256,2048]{1,0:T(8,128)(2,1)S(1)}, bf16[2048,1024]{1,0:T(8,128)(2,1)S(1)}, bf16[2048,1024]{1,0:T(8,128)(2,1)S(1)}) custom-call(bf16[32,4,2048]{2,1,0:T(4,128)(2,1)} %gif_in.3, bf16[32,4,2048]{2,1,0:T(4,128)(2,1)} %uif_in.3, bf16[2048,1024]{1,0:T(8,128)(2,1)} %gw_in.1, bf16[2048,1024]{1,0:T(8,128)(2,1)} %uw_in.1), custom_call_target="tpu_custom_call" | custom-call | flops 2147483648 | bytes 8388608 | tf_op jit(solution)/shard_map/load/pallas_call | solution.py:156
  27.3 0.5 collective-permute-start.22
  28.2 0.7 collective-permute-done.21.refs_5_
  29.0 4.2 %collective-permute-done.8.refs_3_ = bf16[4,24,1024]{2,1,0:T(8,128)(2,1)S(1)} collective-permute-done((bf16[4,24,1024]{2,1,0:T(8,128)(2,1)S(1)}, bf16[4,24,1024]{2,1,0:T(8,128)(2,1)S(1)}, u32[]{:S(2)}, u32[]{:S(2)}) %collective-permute-start.8) | collective-permute-done | bytes 196640 | tf_op jit(solution)/shard_map/ppermute | solution.py:573
  33.2 2.3 %turn.1.in_ref = bf16[2048,256]{1,0:T(8,128)(2,1)S(1)} custom-call(s32[32]{0:T(128)S(1)} %copy-done.1, bf16[32,4,2048]{2,1,0:T(4,128)(2,1)} %gif_in.3, bf16[32,4,2048]{2,1,0:T(4,128)(2,1)} %uif_in.3), custom_call_target="tpu_custom_call" | custom-call | flops 1073741824 | bytes 2097152 | tf_op jit(solution)/shard_map/turn/pallas_call | solution.py:204
  35.5 2.2 %gate_up.5 = (bf16[64,2176]{1,0:T(8,128)(2,1)S(1)}, f32[64,2048]{1,0:T(8,128)S(1)}, bf16[64,128]{1,0:T(8,128)(2,1)S(1)}) custom-call(bf16[32,2048]{1,0:T(8,128)(2,1)S(1)} %copy-done, bf16[32,2048]{1,0:T(8,128)(2,1)S(1)} %collective-permute-done.30.refs_1_, bf16[32,2048]{1,0:T(8,128)(2,1)S(1)} %collective-permute-done.31.refs_2_, ...), custom_call_target="tpu_custom_call" | custom-call | flops 1073741824 | bytes 8388608 | tf_op jit(solution)/shard_map/gate_up/pallas_call | solution.py:352
  37.9 0.6 collective-permute-start.2
  38.5 2.2 %collective-permute-start.9 = (bf16[96,1024]{1,0:T(8,128)(2,1)S(1)}, bf16[96,1024]{1,0:T(8,128)(2,1)S(1)}, u32[]{:S(2)}, u32[]{:S(2)}) collective-permute-start(bf16[96,1024]{1,0:T(8,128)(2,1)S(1)} %get-tuple-element.47), channel_id=1, source_target_pairs={{0,8},{2,10},{4,12},{6,14},{8,16},{10,18},{12,20},{14,22},{16,24},... | collective-permute-start | bytes 589832 | tf_op jit(solution)/shard_map/ppermute | solution.py:573
  40.7 1.9 %collective-permute-start.10 = (bf16[96,1024]{1,0:T(8,128)(2,1)S(1)}, bf16[96,1024]{1,0:T(8,128)(2,1)S(1)}, u32[]{:S(2)}, u32[]{:S(2)}) collective-permute-start(bf16[96,1024]{1,0:T(8,128)(2,1)S(1)} %get-tuple-element.48), channel_id=1, source_target_pairs={{0,16},{2,18},{4,20},{6,22},{8,24},{10,26},{12,28},{14,30},{16,0},... | collective-permute-start | bytes 589832 | tf_op jit(solution)/shard_map/ppermute | solution.py:573
  42.6 2.9 %collective-permute-start.11 = (bf16[96,1024]{1,0:T(8,128)(2,1)S(1)}, bf16[96,1024]{1,0:T(8,128)(2,1)S(1)}, u32[]{:S(2)}, u32[]{:S(2)}) collective-permute-start(bf16[96,1024]{1,0:T(8,128)(2,1)S(1)} %get-tuple-element.49), channel_id=1, source_target_pairs={{0,24},{2,26},{4,28},{6,30},{8,0},{10,2},{12,4},{14,6},{16,8},{18,... | collective-permute-start | bytes 589832 | tf_op jit(solution)/shard_map/ppermute | solution.py:573
  45.4 3.1 %gate_up.4 = (bf16[128,2176]{1,0:T(8,128)(2,1)S(1)}, f32[128,2048]{1,0:T(8,128)S(1)}, bf16[128,128]{1,0:T(8,128)(2,1)S(1)}) custom-call(bf16[32,2048]{1,0:T(8,128)(2,1)S(1)} %collective-permute-done.16.refs_0_, bf16[32,2048]{1,0:T(8,128)(2,1)S(1)} %collective-permute-done.17.refs_1_, bf16[32,2048]{1,0:T(8,128)(2,1)S(1)} %collective-permute-done.18.refs_2_, ...), custom_call_target="tpu_custom_call" | custom-call | flops 2147483648 | bytes 8388608 | tf_op jit(solution)/shard_map/gate_up/pallas_call | solution.py:352
  48.5 1.6 %collective-permute-start.33 = (bf16[64,2176]{1,0:T(8,128)(2,1)S(1)}, bf16[64,2176]{1,0:T(8,128)(2,1)S(1)}, u32[]{:S(2)}, u32[]{:S(2)}) collective-permute-start(bf16[64,2176]{1,0:T(8,128)(2,1)S(1)} %get-tuple-element.63), channel_id=1, source_target_pairs={{0,1},{1,0},{2,3},{3,2},{4,5},{5,4},{6,7},{7,6},{8,9},{9,8},{10,11... | collective-permute-start | bytes 835592 | tf_op jit(solution)/shard_map/ppermute | solution.py:607
  50.1 0.5 collective-permute-start.24
  50.6 2.2 %gate_up.3 = (bf16[64,2176]{1,0:T(8,128)(2,1)S(1)}, f32[64,2048]{1,0:T(8,128)S(1)}, bf16[64,128]{1,0:T(8,128)(2,1)S(1)}) custom-call(bf16[32,2048]{1,0:T(8,128)(2,1)S(1)} %collective-permute-done.refs_0_, bf16[32,2048]{1,0:T(8,128)(2,1)S(1)} %collective-permute-done.1.refs_1_, bf16[32,2048]{1,0:T(8,128)(2,1)S(1)} %collective-permute-done.2.refs_2_, ...), custom_call_target="tpu_custom_call" | custom-call | flops 1073741824 | bytes 8388608 | tf_op jit(solution)/shard_map/gate_up/pallas_call | solution.py:352
  52.8 1.6 %collective-permute-start.4 = (bf16[64,2176]{1,0:T(8,128)(2,1)S(1)}, bf16[64,2176]{1,0:T(8,128)(2,1)S(1)}, u32[]{:S(2)}, u32[]{:S(2)}) collective-permute-start(bf16[64,2176]{1,0:T(8,128)(2,1)S(1)} %get-tuple-element.41), channel_id=1, source_target_pairs={{0,1},{1,0},{2,3},{3,2},{4,5},{5,4},{6,7},{7,6},{8,9},{9,8},{10,11... | collective-permute-start | bytes 835592 | tf_op jit(solution)/shard_map/ppermute | solution.py:607
  54.4 1.7 %collective-permute-done.10.refs_2_ = bf16[96,1024]{1,0:T(8,128)(2,1)S(1)} collective-permute-done((bf16[96,1024]{1,0:T(8,128)(2,1)S(1)}, bf16[96,1024]{1,0:T(8,128)(2,1)S(1)}, u32[]{:S(2)}, u32[]{:S(2)}) %collective-permute-start.10) | collective-permute-done | bytes 196640 | tf_op jit(solution)/shard_map/ppermute | solution.py:573
  56.1 3.0 %arrange.1 = (bf16[256,1024]{1,0:T(8,128)(2,1)S(1)}, bf16[128,1024]{1,0:T(8,128)(2,1)S(1)}, bf16[1024,128]{1,0:T(8,128)(2,1)S(1)}, bf16[128,2048]{1,0:T(8,128)(2...) custom-call(s32[32]{0:T(128)S(1)} %copy-done.1, bf16[32,4,2048]{2,1,0:T(4,128)(2,1)} %right_in.1, ...), custom_call_target="tpu_custom_call" | custom-call | flops 2147483648 | bytes 8388608 | tf_op jit(solution)/shard_map/arrange/pallas_call | solution.py:248
  59.6 1.7 %collective-permute-start.34 = (bf16[64,1024]{1,0:T(8,128)(2,1)S(1)}, bf16[64,1024]{1,0:T(8,128)(2,1)S(1)}, u32[]{:S(2)}, u32[]{:S(2)}) collective-permute-start(bf16[64,1024]{1,0:T(8,128)(2,1)S(1)} %make_hidden.5.refs_0_), channel_id=1, source_target_pairs={{1,0},{0,1},{3,2},{2,3},{5,4},{4,5},{7,6},{6,7},{9,8},{8,9},{11,10... | collective-permute-start | bytes 393224 | tf_op jit(solution)/shard_map/ppermute | solution.py:614
  61.2 4.2 %shard_map.138 = f32[2048,1024]{1,0:T(8,128)} custom-call(bf16[2048,256]{1,0:T(8,128)(2,1)S(1)} %turn.1.in_ref, bf16[256,1024]{1,0:T(8,128)(2,1)S(1)} %get-tuple-element.50.refs_3_.cols_ref), custom_call_target="tpu_custom_call" | custom-call | flops 4294967296 | bytes 8388608 | tf_op jit(solution)/shard_map/pallas_call | solution.py:505
  65.5 10.5 %collective-permute-done.4.refs_2_ = bf16[64,2176]{1,0:T(8,128)(2,1)S(1)} collective-permute-done((bf16[64,2176]{1,0:T(8,128)(2,1)S(1)}, bf16[64,2176]{1,0:T(8,128)(2,1)S(1)}, u32[]{:S(2)}, u32[]{:S(2)}) %collective-permute-start.4) | collective-permute-done | bytes 278560 | tf_op jit(solution)/shard_map/ppermute | solution.py:607
  76.4 1.6 %collective-permute-start.12 = (bf16[64,1024]{1,0:T(8,128)(2,1)S(1)}, bf16[64,1024]{1,0:T(8,128)(2,1)S(1)}, u32[]{:S(2)}, u32[]{:S(2)}) collective-permute-start(bf16[64,1024]{1,0:T(8,128)(2,1)S(1)} %make_hidden.3.refs_0_), channel_id=1, source_target_pairs={{1,0},{0,1},{3,2},{2,3},{5,4},{4,5},{7,6},{6,7},{9,8},{8,9},{11,10... | collective-permute-start | bytes 393224 | tf_op jit(solution)/shard_map/ppermute | solution.py:614
  78.4 1.2 %down.5 = (bf16[64,2048]{1,0:T(8,128)(2,1)S(1)}, f32[64,2048]{1,0:T(8,128)S(1)}) custom-call(bf16[64,1024]{1,0:T(8,128)(2,1)S(1)} %make_hidden.5.refs_0_, bf16[64,1024]{1,0:T(8,128)(2,1)S(1)} %collective-permute-done.34.refs_1_, bf16[1024,2048]{1,0:T(8,128)(2,1)S(1)} %get-tuple-element.51.refs_2_, bf16[128,1024]{1,0:T(8,128)(2,1)S(1)} %get-tuple-element.52.refs_3_, ...), custom_call_target="tpu_custom_call" | custom-call | flops 536870912 | bytes 4194304 | tf_op jit(solution)/shard_map/down/pallas_call | solution.py:476
  79.7 0.6 make_hidden.4.refs_0_
  80.3 1.6 %collective-permute-start.25 = (bf16[128,1024]{1,0:T(8,128)(2,1)S(1)}, bf16[128,1024]{1,0:T(8,128)(2,1)S(1)}, u32[]{:S(2)}, u32[]{:S(2)}) collective-permute-start(bf16[128,1024]{1,0:T(8,128)(2,1)S(1)} %make_hidden.4.refs_0_), channel_id=1, source_target_pairs={{1,0},{0,1},{3,2},{2,3},{5,4},{4,5},{7,6},{6,7},{9,8},{8,9},{11,10... | collective-permute-start | bytes 786440 | tf_op jit(solution)/shard_map/ppermute | solution.py:614
  81.9 4.2 %shard_map.139 = f32[2048,1024]{1,0:T(8,128)} custom-call(bf16[2048,256]{1,0:T(8,128)(2,1)S(1)} %turn.1.in_ref, bf16[256,1024]{1,0:T(8,128)(2,1)S(1)} %get-tuple-element.50.refs_3_.cols_ref), custom_call_target="tpu_custom_call" | custom-call | flops 4294967296 | bytes 8388608 | tf_op jit(solution)/shard_map/pallas_call | solution.py:505
  86.1 1.2 %down.3 = (bf16[64,2048]{1,0:T(8,128)(2,1)S(1)}, f32[64,2048]{1,0:T(8,128)S(1)}) custom-call(bf16[64,1024]{1,0:T(8,128)(2,1)S(1)} %make_hidden.3.refs_0_, bf16[64,1024]{1,0:T(8,128)(2,1)S(1)} %collective-permute-done.12.refs_1_, bf16[1024,2048]{1,0:T(8,128)(2,1)S(1)} %get-tuple-element.51.refs_2_, bf16[128,1024]{1,0:T(8,128)(2,1)S(1)} %get-tuple-element.52.refs_3_, ...), custom_call_target="tpu_custom_call" | custom-call | flops 536870912 | bytes 4194304 | tf_op jit(solution)/shard_map/down/pallas_call | solution.py:476
  87.6 1.5 %collective-permute-done.25.refs_1_ = bf16[128,1024]{1,0:T(8,128)(2,1)S(1)} collective-permute-done((bf16[128,1024]{1,0:T(8,128)(2,1)S(1)}, bf16[128,1024]{1,0:T(8,128)(2,1)S(1)}, u32[]{:S(2)}, u32[]{:S(2)}) %collective-permute-start.25) | collective-permute-done | bytes 262176 | tf_op jit(solution)/shard_map/ppermute | solution.py:614
  89.0 2.0 %down.4 = (bf16[128,2048]{1,0:T(8,128)(2,1)S(1)}, f32[128,2048]{1,0:T(8,128)S(1)}) custom-call(bf16[128,1024]{1,0:T(8,128)(2,1)S(1)} %make_hidden.4.refs_0_, bf16[128,1024]{1,0:T(8,128)(2,1)S(1)} %collective-permute-done.25.refs_1_, bf16[1024,2048]{1,0:T(8,128)(2,1)S(1)} %get-tuple-element.51.refs_2_, bf16[128,1024]{1,0:T(8,128)(2,1)S(1)} %get-tuple-element.52.refs_3_, ...), custom_call_target="tpu_custom_call" | custom-call | flops 1073741824 | bytes 4194304 | tf_op jit(solution)/shard_map/down/pallas_call | solution.py:476
  91.3 1.6 %collective-permute-start.36 = (bf16[32,2048]{1,0:T(8,128)(2,1)S(1)}, bf16[32,2048]{1,0:T(8,128)(2,1)S(1)}, u32[]{:S(2)}, u32[]{:S(2)}) collective-permute-start(bf16[32,2048]{1,0:T(8,128)(2,1)S(1)} %slice.60), channel_id=1, source_target_pairs={{0,4},{2,6},{4,0},{6,2},{8,12},{10,14},{12,8},{14,10},{16,20},{18,... | collective-permute-start | bytes 393224 | tf_op jit(solution)/shard_map/ppermute | solution.py:573
  92.9 0.6 collective-permute-start.14
  93.7 1.6 %collective-permute-start.27 = (bf16[64,2048]{1,0:T(8,128)(2,1)S(1)}, bf16[64,2048]{1,0:T(8,128)(2,1)S(1)}, u32[]{:S(2)}, u32[]{:S(2)}) collective-permute-start(bf16[64,2048]{1,0:T(8,128)(2,1)S(1)} %slice.59), channel_id=1, source_target_pairs={{0,4},{2,6},{4,0},{6,2},{8,12},{10,14},{12,8},{14,10},{16,20},{18,... | collective-permute-start | bytes 786440 | tf_op jit(solution)/shard_map/ppermute | solution.py:573
  95.2 5.3 %collective-permute-done.14 = bf16[32,2048]{1,0:T(8,128)(2,1)S(1)} collective-permute-done((bf16[32,2048]{1,0:T(8,128)(2,1)S(1)}, bf16[32,2048]{1,0:T(8,128)(2,1)S(1)}, u32[]{:S(2)}, u32[]{:S(2)}) %collective-permute-start.14) | collective-permute-done | bytes 131104 | tf_op jit(solution)/shard_map/ppermute | solution.py:573
  100.6 5.0 %collective-permute-done.27 = bf16[64,2048]{1,0:T(8,128)(2,1)S(1)} collective-permute-done((bf16[64,2048]{1,0:T(8,128)(2,1)S(1)}, bf16[64,2048]{1,0:T(8,128)(2,1)S(1)}, u32[]{:S(2)}, u32[]{:S(2)}) %collective-permute-start.27) | collective-permute-done | bytes 262176 | tf_op jit(solution)/shard_map/ppermute | solution.py:573
  105.8 0.6 collective-permute-start.28
  106.4 4.2 %down_step.1 = f32[1024,2048]{1,0:T(8,128)} custom-call(bf16[1024,128]{1,0:T(8,128)(2,1)S(1)} %get-tuple-element.66.left_ref, bf16[128,2048]{1,0:T(8,128)(2,1)S(1)} %get-tuple-element.67.right_ref), custom_call_target="tpu_custom_call" | custom-call | flops 2147483648 | bytes 8388608 | tf_op jit(solution)/shard_map/down_step/pallas_call | solution.py:528
  110.6 0.6 collective-permute-done.29
  111.2 4.6 %collective-permute-done.28 = bf16[32,2048]{1,0:T(8,128)(2,1)S(1)} collective-permute-done((bf16[32,2048]{1,0:T(8,128)(2,1)S(1)}, bf16[32,2048]{1,0:T(8,128)(2,1)S(1)}, u32[]{:S(2)}, u32[]{:S(2)}) %collective-permute-start.28) | collective-permute-done | bytes 131104 | tf_op jit(solution)/shard_map/ppermute | solution.py:573
  115.8 0.7 fusion.2
  (57 shorter events, 4.2 us)
Async XLA Ops:
  0.6 7.8 %collective-permute-start.30 = (bf16[32,2048]{1,0:T(8,128)(2,1)}, bf16[32,2048]{1,0:T(8,128)(2,1)S(1)}, u32[]{:S(2)}, u32[]{:S(2)}) collective-permute-start(bf16[32,2048]{1,0:T(8,128)(2,1)} %refs_0_.1), channel_id=1, source_target_pairs={{0,4},{2,6},{4,0},{6,2},{8,12},{10,14},{12,8},{14,10},{16,20},{18,... | collective-permute-start | bytes 393224 | tf_op jit(solution)/shard_map/ppermute | solution.py:573
  3.7 6.3 %collective-permute-start.31 = (bf16[32,2048]{1,0:T(8,128)(2,1)}, bf16[32,2048]{1,0:T(8,128)(2,1)S(1)}, u32[]{:S(2)}, u32[]{:S(2)}) collective-permute-start(bf16[32,2048]{1,0:T(8,128)(2,1)} %refs_0_.1), channel_id=1, source_target_pairs={{0,2},{2,0},{4,6},{6,4},{8,10},{10,8},{12,14},{14,12},{16,18},{18,... | collective-permute-start | bytes 393224 | tf_op jit(solution)/shard_map/ppermute | solution.py:573
  5.0 16.3 %collective-permute-start.5 = (bf16[4,24,1024]{2,1,0:T(8,128)(2,1)S(1)}, bf16[4,24,1024]{2,1,0:T(8,128)(2,1)S(1)}, u32[]{:S(2)}, u32[]{:S(2)}) collective-permute-start(bf16[4,24,1024]{2,1,0:T(8,128)(2,1)S(1)} %get-tuple-element.43), channel_id=1, source_target_pairs={{0,4},{2,6},{4,0},{6,2},{8,12},{10,14},{12,8},{14,10},{16,20},{18,... | collective-permute-start | bytes 589832 | tf_op jit(solution)/shard_map/ppermute | solution.py:573
  5.1 16.7 %collective-permute-start.7 = (bf16[4,24,1024]{2,1,0:T(8,128)(2,1)S(1)}, bf16[4,24,1024]{2,1,0:T(8,128)(2,1)S(1)}, u32[]{:S(2)}, u32[]{:S(2)}) collective-permute-start(bf16[4,24,1024]{2,1,0:T(8,128)(2,1)S(1)} %get-tuple-element.45), channel_id=1, source_target_pairs={{0,2},{2,0},{4,6},{6,4},{8,10},{10,8},{12,14},{14,12},{16,18},{18,... | collective-permute-start | bytes 589832 | tf_op jit(solution)/shard_map/ppermute | solution.py:573
  5.6 13.1 %collective-permute-start.16 = (bf16[32,2048]{1,0:T(8,128)(2,1)}, bf16[32,2048]{1,0:T(8,128)(2,1)S(1)}, u32[]{:S(2)}, u32[]{:S(2)}) collective-permute-start(bf16[32,2048]{1,0:T(8,128)(2,1)} %refs_0_.1), channel_id=1, source_target_pairs={{0,16},{2,18},{4,20},{6,22},{8,24},{10,26},{12,28},{14,30},{16,0},... | collective-permute-start | bytes 393224 | tf_op jit(solution)/shard_map/ppermute | solution.py:573
  8.4 10.4 %collective-permute-start.20 = (bf16[32,2048]{1,0:T(8,128)(2,1)}, bf16[32,2048]{1,0:T(8,128)(2,1)S(1)}, u32[]{:S(2)}, u32[]{:S(2)}) collective-permute-start(bf16[32,2048]{1,0:T(8,128)(2,1)} %refs_0_.1), channel_id=1, source_target_pairs={{0,8},{2,10},{4,12},{6,14},{8,16},{10,18},{12,20},{14,22},{16,24},... | collective-permute-start | bytes 393224 | tf_op jit(solution)/shard_map/ppermute | solution.py:573
  10.0 9.8 %collective-permute-start = (bf16[32,2048]{1,0:T(8,128)(2,1)}, bf16[32,2048]{1,0:T(8,128)(2,1)S(1)}, u32[]{:S(2)}, u32[]{:S(2)}) collective-permute-start(bf16[32,2048]{1,0:T(8,128)(2,1)} %refs_0_.1), channel_id=1, source_target_pairs={{0,24},{2,26},{4,28},{6,30},{8,0},{10,2},{12,4},{14,6},{16,8},{18,... | collective-permute-start | bytes 393224 | tf_op jit(solution)/shard_map/ppermute | solution.py:573
  18.8 14.4 %copy-start.1 = (s32[32]{0:T(128)S(1)}, s32[32]{0:T(128)}, u32[]{:S(2)}) copy-start(s32[32]{0:T(128)} %ranks_ref.3) | copy-start | bytes 388
  18.8 16.7 %copy-start = (bf16[32,2048]{1,0:T(8,128)(2,1)S(1)}, bf16[32,2048]{1,0:T(8,128)(2,1)}, u32[]{:S(2)}) copy-start(bf16[32,2048]{1,0:T(8,128)(2,1)} %refs_0_.1) | copy-start | bytes 393220
  18.8 8.4 %collective-permute-start.6 = (bf16[4,24,1024]{2,1,0:T(8,128)(2,1)S(1)}, bf16[4,24,1024]{2,1,0:T(8,128)(2,1)S(1)}, u32[]{:S(2)}, u32[]{:S(2)}) collective-permute-start(bf16[4,24,1024]{2,1,0:T(8,128)(2,1)S(1)} %get-tuple-element.44), channel_id=1, source_target_pairs={{0,2},{2,0},{4,6},{6,4},{8,10},{10,8},{12,14},{14,12},{16,18},{18,... | collective-permute-start | bytes 589832 | tf_op jit(solution)/shard_map/ppermute | solution.py:573
  18.8 8.5 %collective-permute-start.32 = (bf16[32,2048]{1,0:T(8,128)(2,1)S(1)}, bf16[32,2048]{1,0:T(8,128)(2,1)S(1)}, u32[]{:S(2)}, u32[]{:S(2)}) collective-permute-start(bf16[32,2048]{1,0:T(8,128)(2,1)S(1)} %collective-permute-done.30.refs_1_), channel_id=1, source_target_pairs={{0,2},{2,0},{4,6},{6,4},{8,10},{10,8},{12,14},{14,12},{16,18},{18,... | collective-permute-start | bytes 393224 | tf_op jit(solution)/shard_map/ppermute | solution.py:573
  19.8 8.0 %collective-permute-start.17 = (bf16[32,2048]{1,0:T(8,128)(2,1)S(1)}, bf16[32,2048]{1,0:T(8,128)(2,1)S(1)}, u32[]{:S(2)}, u32[]{:S(2)}) collective-permute-start(bf16[32,2048]{1,0:T(8,128)(2,1)S(1)} %collective-permute-done.16.refs_0_), channel_id=1, source_target_pairs={{0,4},{2,6},{4,0},{6,2},{8,12},{10,14},{12,8},{14,10},{16,20},{18,... | collective-permute-start | bytes 393224 | tf_op jit(solution)/shard_map/ppermute | solution.py:573
  21.3 7.6 %collective-permute-start.21 = (bf16[32,2048]{1,0:T(8,128)(2,1)S(1)}, bf16[32,2048]{1,0:T(8,128)(2,1)S(1)}, u32[]{:S(2)}, u32[]{:S(2)}) collective-permute-start(bf16[32,2048]{1,0:T(8,128)(2,1)S(1)} %collective-permute-done.20.refs_4_), channel_id=1, source_target_pairs={{0,4},{2,6},{4,0},{6,2},{8,12},{10,14},{12,8},{14,10},{16,20},{18,... | collective-permute-start | bytes 393224 | tf_op jit(solution)/shard_map/ppermute | solution.py:573
  21.8 11.3 %collective-permute-start.8 = (bf16[4,24,1024]{2,1,0:T(8,128)(2,1)S(1)}, bf16[4,24,1024]{2,1,0:T(8,128)(2,1)S(1)}, u32[]{:S(2)}, u32[]{:S(2)}) collective-permute-start(bf16[4,24,1024]{2,1,0:T(8,128)(2,1)S(1)} %collective-permute-done.7), channel_id=1, source_target_pairs={{0,4},{2,6},{4,0},{6,2},{8,12},{10,14},{12,8},{14,10},{16,20},{18,... | collective-permute-start | bytes 589832 | tf_op jit(solution)/shard_map/ppermute | solution.py:573
  27.2 10.7 %collective-permute-start.18 = (bf16[32,2048]{1,0:T(8,128)(2,1)S(1)}, bf16[32,2048]{1,0:T(8,128)(2,1)S(1)}, u32[]{:S(2)}, u32[]{:S(2)}) collective-permute-start(bf16[32,2048]{1,0:T(8,128)(2,1)S(1)} %collective-permute-done.16.refs_0_), channel_id=1, source_target_pairs={{0,2},{2,0},{4,6},{6,4},{8,10},{10,8},{12,14},{14,12},{16,18},{18,... | collective-permute-start | bytes 393224 | tf_op jit(solution)/shard_map/ppermute | solution.py:573
  27.3 11.3 %collective-permute-start.22 = (bf16[32,2048]{1,0:T(8,128)(2,1)S(1)}, bf16[32,2048]{1,0:T(8,128)(2,1)S(1)}, u32[]{:S(2)}, u32[]{:S(2)}) collective-permute-start(bf16[32,2048]{1,0:T(8,128)(2,1)S(1)} %collective-permute-done.20.refs_4_), channel_id=1, source_target_pairs={{0,2},{2,0},{4,6},{6,4},{8,10},{10,8},{12,14},{14,12},{16,18},{18,... | collective-permute-start | bytes 393224 | tf_op jit(solution)/shard_map/ppermute | solution.py:573
  27.8 10.7 %collective-permute-start.1 = (bf16[32,2048]{1,0:T(8,128)(2,1)S(1)}, bf16[32,2048]{1,0:T(8,128)(2,1)S(1)}, u32[]{:S(2)}, u32[]{:S(2)}) collective-permute-start(bf16[32,2048]{1,0:T(8,128)(2,1)S(1)} %collective-permute-done.refs_0_), channel_id=1, source_target_pairs={{0,4},{2,6},{4,0},{6,2},{8,12},{10,14},{12,8},{14,10},{16,20},{18,... | collective-permute-start | bytes 393224 | tf_op jit(solution)/shard_map/ppermute | solution.py:573
  29.0 11.7 %collective-permute-start.19 = (bf16[32,2048]{1,0:T(8,128)(2,1)S(1)}, bf16[32,2048]{1,0:T(8,128)(2,1)S(1)}, u32[]{:S(2)}, u32[]{:S(2)}) collective-permute-start(bf16[32,2048]{1,0:T(8,128)(2,1)S(1)} %collective-permute-done.17.refs_1_), channel_id=1, source_target_pairs={{0,2},{2,0},{4,6},{6,4},{8,10},{10,8},{12,14},{14,12},{16,18},{18,... | collective-permute-start | bytes 393224 | tf_op jit(solution)/shard_map/ppermute | solution.py:573
  33.2 9.4 %collective-permute-start.23 = (bf16[32,2048]{1,0:T(8,128)(2,1)S(1)}, bf16[32,2048]{1,0:T(8,128)(2,1)S(1)}, u32[]{:S(2)}, u32[]{:S(2)}) collective-permute-start(bf16[32,2048]{1,0:T(8,128)(2,1)S(1)} %collective-permute-done.21.refs_5_), channel_id=1, source_target_pairs={{0,2},{2,0},{4,6},{6,4},{8,10},{10,8},{12,14},{14,12},{16,18},{18,... | collective-permute-start | bytes 393224 | tf_op jit(solution)/shard_map/ppermute | solution.py:573
  37.9 10.6 %collective-permute-start.2 = (bf16[32,2048]{1,0:T(8,128)(2,1)S(1)}, bf16[32,2048]{1,0:T(8,128)(2,1)S(1)}, u32[]{:S(2)}, u32[]{:S(2)}) collective-permute-start(bf16[32,2048]{1,0:T(8,128)(2,1)S(1)} %collective-permute-done.refs_0_), channel_id=1, source_target_pairs={{0,2},{2,0},{4,6},{6,4},{8,10},{10,8},{12,14},{14,12},{16,18},{18,... | collective-permute-start | bytes 393224 | tf_op jit(solution)/shard_map/ppermute | solution.py:573
  38.4 11.6 %collective-permute-start.3 = (bf16[32,2048]{1,0:T(8,128)(2,1)S(1)}, bf16[32,2048]{1,0:T(8,128)(2,1)S(1)}, u32[]{:S(2)}, u32[]{:S(2)}) collective-permute-start(bf16[32,2048]{1,0:T(8,128)(2,1)S(1)} %collective-permute-done.1.refs_1_), channel_id=1, source_target_pairs={{0,2},{2,0},{4,6},{6,4},{8,10},{10,8},{12,14},{14,12},{16,18},{18,... | collective-permute-start | bytes 393224 | tf_op jit(solution)/shard_map/ppermute | solution.py:573
  38.5 14.3 %collective-permute-start.9 = (bf16[96,1024]{1,0:T(8,128)(2,1)S(1)}, bf16[96,1024]{1,0:T(8,128)(2,1)S(1)}, u32[]{:S(2)}, u32[]{:S(2)}) collective-permute-start(bf16[96,1024]{1,0:T(8,128)(2,1)S(1)} %get-tuple-element.47), channel_id=1, source_target_pairs={{0,8},{2,10},{4,12},{6,14},{8,16},{10,18},{12,20},{14,22},{16,24},... | collective-permute-start | bytes 589832 | tf_op jit(solution)/shard_map/ppermute | solution.py:573
  40.7 15.4 %collective-permute-start.10 = (bf16[96,1024]{1,0:T(8,128)(2,1)S(1)}, bf16[96,1024]{1,0:T(8,128)(2,1)S(1)}, u32[]{:S(2)}, u32[]{:S(2)}) collective-permute-start(bf16[96,1024]{1,0:T(8,128)(2,1)S(1)} %get-tuple-element.48), channel_id=1, source_target_pairs={{0,16},{2,18},{4,20},{6,22},{8,24},{10,26},{12,28},{14,30},{16,0},... | collective-permute-start | bytes 589832 | tf_op jit(solution)/shard_map/ppermute | solution.py:573
  42.6 13.5 %collective-permute-start.11 = (bf16[96,1024]{1,0:T(8,128)(2,1)S(1)}, bf16[96,1024]{1,0:T(8,128)(2,1)S(1)}, u32[]{:S(2)}, u32[]{:S(2)}) collective-permute-start(bf16[96,1024]{1,0:T(8,128)(2,1)S(1)} %get-tuple-element.49), channel_id=1, source_target_pairs={{0,24},{2,26},{4,28},{6,30},{8,0},{10,2},{12,4},{14,6},{16,8},{18,... | collective-permute-start | bytes 589832 | tf_op jit(solution)/shard_map/ppermute | solution.py:573
  48.5 10.6 %collective-permute-start.33 = (bf16[64,2176]{1,0:T(8,128)(2,1)S(1)}, bf16[64,2176]{1,0:T(8,128)(2,1)S(1)}, u32[]{:S(2)}, u32[]{:S(2)}) collective-permute-start(bf16[64,2176]{1,0:T(8,128)(2,1)S(1)} %get-tuple-element.63), channel_id=1, source_target_pairs={{0,1},{1,0},{2,3},{3,2},{4,5},{5,4},{6,7},{7,6},{8,9},{9,8},{10,11... | collective-permute-start | bytes 835592 | tf_op jit(solution)/shard_map/ppermute | solution.py:607
  50.1 29.6 %collective-permute-start.24 = (bf16[128,2176]{1,0:T(8,128)(2,1)S(1)}, bf16[128,2176]{1,0:T(8,128)(2,1)S(1)}, u32[]{:S(2)}, u32[]{:S(2)}) collective-permute-start(bf16[128,2176]{1,0:T(8,128)(2,1)S(1)} %get-tuple-element.58), channel_id=1, source_target_pairs={{0,1},{1,0},{2,3},{3,2},{4,5},{5,4},{6,7},{7,6},{8,9},{9,8},{10,11... | collective-permute-start | bytes 1671176 | tf_op jit(solution)/shard_map/ppermute | solution.py:607
  52.8 23.2 %collective-permute-start.4 = (bf16[64,2176]{1,0:T(8,128)(2,1)S(1)}, bf16[64,2176]{1,0:T(8,128)(2,1)S(1)}, u32[]{:S(2)}, u32[]{:S(2)}) collective-permute-start(bf16[64,2176]{1,0:T(8,128)(2,1)S(1)} %get-tuple-element.41), channel_id=1, source_target_pairs={{0,1},{1,0},{2,3},{3,2},{4,5},{5,4},{6,7},{7,6},{8,9},{9,8},{10,11... | collective-permute-start | bytes 835592 | tf_op jit(solution)/shard_map/ppermute | solution.py:607
  59.6 18.8 %collective-permute-start.34 = (bf16[64,1024]{1,0:T(8,128)(2,1)S(1)}, bf16[64,1024]{1,0:T(8,128)(2,1)S(1)}, u32[]{:S(2)}, u32[]{:S(2)}) collective-permute-start(bf16[64,1024]{1,0:T(8,128)(2,1)S(1)} %make_hidden.5.refs_0_), channel_id=1, source_target_pairs={{1,0},{0,1},{3,2},{2,3},{5,4},{4,5},{7,6},{6,7},{9,8},{8,9},{11,10... | collective-permute-start | bytes 393224 | tf_op jit(solution)/shard_map/ppermute | solution.py:614
  76.4 9.6 %collective-permute-start.12 = (bf16[64,1024]{1,0:T(8,128)(2,1)S(1)}, bf16[64,1024]{1,0:T(8,128)(2,1)S(1)}, u32[]{:S(2)}, u32[]{:S(2)}) collective-permute-start(bf16[64,1024]{1,0:T(8,128)(2,1)S(1)} %make_hidden.3.refs_0_), channel_id=1, source_target_pairs={{1,0},{0,1},{3,2},{2,3},{5,4},{4,5},{7,6},{6,7},{9,8},{8,9},{11,10... | collective-permute-start | bytes 393224 | tf_op jit(solution)/shard_map/ppermute | solution.py:614
  79.6 11.6 %collective-permute-start.35 = (bf16[64,2048]{1,0:T(8,128)(2,1)S(1)}, bf16[64,2048]{1,0:T(8,128)(2,1)S(1)}, u32[]{:S(2)}, u32[]{:S(2)}) collective-permute-start(bf16[64,2048]{1,0:T(8,128)(2,1)S(1)} %get-tuple-element.65), channel_id=1, source_target_pairs={{0,2},{2,0},{4,6},{6,4},{8,10},{10,8},{12,14},{14,12},{16,18},{18,... | collective-permute-start | bytes 786440 | tf_op jit(solution)/shard_map/ppermute | solution.py:573
  80.3 8.8 %collective-permute-start.25 = (bf16[128,1024]{1,0:T(8,128)(2,1)S(1)}, bf16[128,1024]{1,0:T(8,128)(2,1)S(1)}, u32[]{:S(2)}, u32[]{:S(2)}) collective-permute-start(bf16[128,1024]{1,0:T(8,128)(2,1)S(1)} %make_hidden.4.refs_0_), channel_id=1, source_target_pairs={{1,0},{0,1},{3,2},{2,3},{5,4},{4,5},{7,6},{6,7},{9,8},{8,9},{11,10... | collective-permute-start | bytes 786440 | tf_op jit(solution)/shard_map/ppermute | solution.py:614
  87.3 5.6 %collective-permute-start.13 = (bf16[64,2048]{1,0:T(8,128)(2,1)S(1)}, bf16[64,2048]{1,0:T(8,128)(2,1)S(1)}, u32[]{:S(2)}, u32[]{:S(2)}) collective-permute-start(bf16[64,2048]{1,0:T(8,128)(2,1)S(1)} %get-tuple-element.55), channel_id=1, source_target_pairs={{0,2},{2,0},{4,6},{6,4},{8,10},{10,8},{12,14},{14,12},{16,18},{18,... | collective-permute-start | bytes 786440 | tf_op jit(solution)/shard_map/ppermute | solution.py:573
  91.1 2.4 %collective-permute-start.26 = (bf16[128,2048]{1,0:T(8,128)(2,1)S(1)}, bf16[128,2048]{1,0:T(8,128)(2,1)S(1)}, u32[]{:S(2)}, u32[]{:S(2)}) collective-permute-start(bf16[128,2048]{1,0:T(8,128)(2,1)S(1)} %get-tuple-element.60), channel_id=1, source_target_pairs={{0,2},{2,0},{4,6},{6,4},{8,10},{10,8},{12,14},{14,12},{16,18},{18,... | collective-permute-start | bytes 1572872 | tf_op jit(solution)/shard_map/ppermute | solution.py:573
  91.3 19.3 %collective-permute-start.36 = (bf16[32,2048]{1,0:T(8,128)(2,1)S(1)}, bf16[32,2048]{1,0:T(8,128)(2,1)S(1)}, u32[]{:S(2)}, u32[]{:S(2)}) collective-permute-start(bf16[32,2048]{1,0:T(8,128)(2,1)S(1)} %slice.60), channel_id=1, source_target_pairs={{0,4},{2,6},{4,0},{6,2},{8,12},{10,14},{12,8},{14,10},{16,20},{18,... | collective-permute-start | bytes 393224 | tf_op jit(solution)/shard_map/ppermute | solution.py:573
  92.9 7.6 %collective-permute-start.14 = (bf16[32,2048]{1,0:T(8,128)(2,1)S(1)}, bf16[32,2048]{1,0:T(8,128)(2,1)S(1)}, u32[]{:S(2)}, u32[]{:S(2)}) collective-permute-start(bf16[32,2048]{1,0:T(8,128)(2,1)S(1)} %slice.61), channel_id=1, source_target_pairs={{0,4},{2,6},{4,0},{6,2},{8,12},{10,14},{12,8},{14,10},{16,20},{18,... | collective-permute-start | bytes 393224 | tf_op jit(solution)/shard_map/ppermute | solution.py:573
  93.7 12.0 %collective-permute-start.27 = (bf16[64,2048]{1,0:T(8,128)(2,1)S(1)}, bf16[64,2048]{1,0:T(8,128)(2,1)S(1)}, u32[]{:S(2)}, u32[]{:S(2)}) collective-permute-start(bf16[64,2048]{1,0:T(8,128)(2,1)S(1)} %slice.59), channel_id=1, source_target_pairs={{0,4},{2,6},{4,0},{6,2},{8,12},{10,14},{12,8},{14,10},{16,20},{18,... | collective-permute-start | bytes 786440 | tf_op jit(solution)/shard_map/ppermute | solution.py:573
  100.5 10.1 %collective-permute-start.15 = (bf16[32,2048]{1,0:T(8,128)(2,1)S(1)}, bf16[32,2048]{1,0:T(8,128)(2,1)S(1)}, u32[]{:S(2)}, u32[]{:S(2)}) collective-permute-start(bf16[32,2048]{1,0:T(8,128)(2,1)S(1)} %fusion.3), channel_id=1, source_target_pairs={{0,8},{2,10},{4,12},{6,14},{8,16},{10,18},{12,20},{14,22},{16,24},... | collective-permute-start | bytes 393224 | tf_op jit(solution)/shard_map/ppermute | solution.py:573
  105.7 5.4 %collective-permute-start.29 = (bf16[32,2048]{1,0:T(8,128)(2,1)S(1)}, bf16[32,2048]{1,0:T(8,128)(2,1)S(1)}, u32[]{:S(2)}, u32[]{:S(2)}) collective-permute-start(bf16[32,2048]{1,0:T(8,128)(2,1)S(1)} %get-tuple-element.69), channel_id=1, source_target_pairs={{0,24},{2,26},{4,28},{6,30},{8,0},{10,2},{12,4},{14,6},{16,8},{18,... | collective-permute-start | bytes 393224 | tf_op jit(solution)/shard_map/ppermute | solution.py:573
  105.8 10.0 %collective-permute-start.28 = (bf16[32,2048]{1,0:T(8,128)(2,1)S(1)}, bf16[32,2048]{1,0:T(8,128)(2,1)S(1)}, u32[]{:S(2)}, u32[]{:S(2)}) collective-permute-start(bf16[32,2048]{1,0:T(8,128)(2,1)S(1)} %get-tuple-element.68), channel_id=1, source_target_pairs={{0,16},{2,18},{4,20},{6,22},{8,24},{10,26},{12,28},{14,30},{16,0},... | collective-permute-start | bytes 393224 | tf_op jit(solution)/shard_map/ppermute | solution.py:573
where the time goes:
time: 117 us
  waiting for transfers between devices  41.5 us (35%)
  Pallas kernels  36.6 us (31%)
  starting transfers between devices  36.3 us (31%)
    ppermute x31, waiting for transfers between devices, along(): return lax.ppermute(v, 'pop', pairs)  29.1 us
    ppermute x31, starting transfers between devices, along(): return lax.ppermute(v, 'pop', pairs)  27.8 us
    ppermute x3, waiting for transfers between devices, local(): lax.ppermute(v, 'hid', [(i, (i + s + 1) % hid_count) for i in range(hid_c...  10.5 us
    pallas_call x2, Pallas kernels, input_step(): pl.pallas_call(functools.partial(input_step_kernel, index, group, factor)...  8.42 us
    pallas_call x3, Pallas kernels, gate_up(): pl.pallas_call(functools.partial(gate_up_kernel, shifts, z_count, hid_cou...  7.54 us
    ppermute x3, starting transfers between devices, local(): lax.ppermute(mine, 'hid', [((i + s) % hid_count, i) for i in range(hid_co...  4.82 us
    pallas_call x3, Pallas kernels, down(): pl.pallas_call(functools.partial(down_kernel, shifts, z_count, hid_count,...  4.42 us
    pallas_call x1, Pallas kernels, down_step(): pl.pallas_call(functools.partial(down_step_kernel, factor), grid=(hidden...  4.16 us
  transfers between devices with their start and end apart: 37, of which 12 were waited for; matrix products, arithmetic and copies ran while one was open for 0% of the time, Pallas kernels for 31%

commit v1 on v0

--- a/solution.py
+++ b/solution.py
@@ -82,7 +82,7 @@
     for q in range(PLANE):
         xs, cs = jnp.bitwise_xor(x, q % X_COUNT), jnp.bitwise_xor(c, q // X_COUNT)
         for k in range(z_count):
-            to = (lax.rem(z + k, z_count) * X_COUNT + xs) * CORE_COUNT + cs
+            to = (jnp.bitwise_xor(z, k) * X_COUNT + xs) * CORE_COUNT + cs
             at = pl.ds(pl.multiple_of(to * part, LANES), part)
             rows = [ref[m, :, at].astype(F32) for ref in parts for m in range(mem)]
             outs[q][k] = jnp.concatenate(rows, axis=0).astype(BF16)
@@ -225,7 +225,7 @@
     third = gots[0].shape[0] // 3
     members = raw_ref.shape[0]
     for k, got in enumerate(gots):
-        zs = lax.rem(z - k + z_count, z_count)
+        zs = jnp.bitwise_xor(z, k)
         gu_ref[pl.ds(pl.multiple_of(zs * 2 * third, 2 * third), 2 * third), :] = got[: 2 * third, :]
         down_at = pl.ds(pl.multiple_of(zs * third, third), third)
         d_ref[down_at, :] = got[2 * third :, :]
@@ -270,13 +270,13 @@
     )(ranks, *fixed(right, dw), *gots)
 
 
-def unit_members(units, per_block, shifts, z, z_count, start):
+def unit_members(units, per_block, shifts, z, start):
     members = []
     for w in range(units):
         unit = start(w)
         zs = jnp.int32(0)
         for b, shift in enumerate(shifts):
-            zs = jnp.where(unit // per_block == b, lax.rem(z + shift, z_count), zs)
+            zs = jnp.where(unit // per_block == b, jnp.bitwise_xor(z, shift), zs)
         members.append(zs * per_block + unit % per_block)
     return members
 
@@ -286,7 +286,7 @@
     return lane // (2 * group) * (group // RANK) + lane % group // RANK
 
 
-def gate_up_kernel(shifts, z_count, hid_count, mem_local, *refs):
+def gate_up_kernel(shifts, hid_count, mem_local, *refs):
     blocks = len(shifts)
     pieces = refs[: PLANE * blocks]
     gw_ref, uw_ref, giu_ref = refs[PLANE * blocks : PLANE * blocks + 3]
@@ -317,7 +317,6 @@
         per_block,
         shifts,
         z,
-        z_count,
         lambda p: lax.rem(p // per_part + y + 1, hid_count) * per_part + p % per_part,
     )
     rows = rows_ref[...]
@@ -343,16 +342,14 @@
             keep_ref[:, at] = value[(hid_count - 1) * part_rows :]
 
 
-def gate_up(pieces, gw, uw, giu, shifts, z_count, hid_count):
+def gate_up(pieces, gw, uw, giu, shifts, hid_count):
     rows, width = pieces[0].shape
     hidden = gw.shape[1]
     total = rows * PLANE * len(shifts)
     part = total // hid_count
     send_shape = (part, 2 * hidden + LANES)
     return pl.pallas_call(
-        functools.partial(
-            gate_up_kernel, shifts, z_count, hid_count, rows // SAMPLE_LENGTH
-        ),
+        functools.partial(gate_up_kernel, shifts, hid_count, rows // SAMPLE_LENGTH),
         in_specs=[IN_VMEM] * (len(pieces) + 3),
         out_specs=[IN_VMEM] * (hid_count + 1),
         out_shape=[jax.ShapeDtypeStruct(send_shape, BF16)] * (hid_count - 1)
@@ -369,7 +366,7 @@
     )(*pieces, gw, uw, giu)
 
 
-def hidden_kernel(shifts, z_count, hid_count, mem_local, scale, *refs):
+def hidden_kernel(shifts, hid_count, mem_local, scale, *refs):
     keep_ref, keep_proj = refs[:2]
     recvs = refs[2 : 1 + hid_count]
     cols_ref, out_ref = refs[1 + hid_count :]
@@ -379,9 +376,7 @@
     lanes, hidden = cols_ref.shape
     group = mem_local * RANK
     rows = keep_proj.shape[0]
-    members = unit_members(
-        per_part, per_block, shifts, z, z_count, lambda w: y * per_part + w
-    )
+    members = unit_members(per_part, per_block, shifts, z, lambda w: y * per_part + w)
     mine = row_members((rows, lanes), members) == lane_members((rows, lanes), group)
     source, target = iota((LANES, lanes), 0), iota((LANES, lanes), 1)
     base = target % RANK + 2 * RANK * (target // group % 2)
@@ -412,12 +407,12 @@
         ).astype(BF16)
 
 
-def make_hidden(keep, keep_proj, recvs, cols, shifts, z_count, hid_count, mem_local, scale):
+def make_hidden(keep, keep_proj, recvs, cols, shifts, hid_count, mem_local, scale):
     part = keep.shape[0]
     hidden = keep.shape[1] // 2
     lanes = cols.shape[0]
     return pl.pallas_call(
-        functools.partial(hidden_kernel, shifts, z_count, hid_count, mem_local, scale),
+        functools.partial(hidden_kernel, shifts, hid_count, mem_local, scale),
         in_specs=[IN_VMEM] * (3 + len(recvs)),
         out_specs=IN_VMEM,
         out_shape=jax.ShapeDtypeStruct((part, hidden), BF16),
@@ -429,7 +424,7 @@
     )(keep, keep_proj, *recvs, cols)
 
 
-def down_kernel(shifts, z_count, hid_count, mem_local, scale, *refs):
+def down_kernel(shifts, hid_count, mem_local, scale, *refs):
     blocks = len(shifts)
     parts = refs[:hid_count]
     dw_ref, cols_ref, right_ref, send_ref, keep_ref, rows_ref = refs[hid_count:]
@@ -454,7 +449,7 @@
         q, b = slot // blocks, slot % blocks
         xs = jnp.bitwise_xor(x, 1 - q % X_COUNT)
         cs = jnp.bitwise_xor(c, 1 - q // X_COUNT)
-        zs = lax.rem(z + shifts[b], z_count)
+        zs = jnp.bitwise_xor(z, shifts[b])
         members.append(((zs * X_COUNT + xs) * CORE_COUNT + cs) * mem_local + m)
     rows = rows_ref[...]
     projected = dot_nt(rows, cols_ref[...])
@@ -469,12 +464,12 @@
         keep_ref[:, at] = value[half:]
 
 
-def down(parts, dw, cols, right, shifts, z_count, hid_count, mem_local, scale):
+def down(parts, dw, cols, right, shifts, hid_count, mem_local, scale):
     part, hidden = parts[0].shape
     width = dw.shape[1]
     total = part * hid_count
     return pl.pallas_call(
-        functools.partial(down_kernel, shifts, z_count, hid_count, mem_local, scale),
+        functools.partial(down_kernel, shifts, hid_count, mem_local, scale),
         in_specs=[IN_VMEM] * (hid_count + 3),
         out_specs=[IN_VMEM] * 2,
         out_shape=[
@@ -555,6 +550,7 @@
     pop_count = lax.axis_size("pop")
     hid_count = lax.axis_size("hid")
     z_count = pop_count // PLANE
+    assert z_count & (z_count - 1) == 0
     tok_local, _ = tokens.shape
     mem_local = tok_local // SAMPLE_LENGTH
     members = mem_local * pop_count
@@ -567,7 +563,7 @@
     x_pairs = [(i, i ^ CORE_COUNT) for i in everyone]
 
     def forward(k):
-        return [(i, (i + k * PLANE) % pop_count) for i in everyone]
+        return [(i, i ^ (k * PLANE)) for i in everyone]
 
     def along(v, pairs):
         return lax.ppermute(v, "pop", pairs)
@@ -576,7 +572,7 @@
 
     blocks = {}
     for k in range(z_count):
-        own = tokens if k == 0 else along(tokens, forward(z_count - k))
+        own = tokens if k == 0 else along(tokens, forward(k))
         from_x = along(own, x_pairs)
         from_core = along(own, core_pairs)
         from_both = along(from_x, core_pairs)
@@ -600,23 +596,17 @@
     total = None
     for shifts in groups:
         pieces = [piece for k in shifts for piece in blocks[k]]
-        *sends, keep, keep_proj = gate_up(
-            pieces, gate_v, up_v, giu, shifts, z_count, hid_count
-        )
+        *sends, keep, keep_proj = gate_up(pieces, gate_v, up_v, giu, shifts, hid_count)
         recvs = [
             lax.ppermute(v, "hid", [(i, (i + s + 1) % hid_count) for i in range(hid_count)])
             for s, v in enumerate(sends)
         ]
-        mine = make_hidden(
-            keep, keep_proj, recvs, gu_cols, shifts, z_count, hid_count, mem_local, scale_in
-        )
+        mine = make_hidden(keep, keep_proj, recvs, gu_cols, shifts, hid_count, mem_local, scale_in)
         parts = [mine] + [
             lax.ppermute(mine, "hid", [((i + s) % hid_count, i) for i in range(hid_count)])
             for s in range(1, hid_count)
         ]
-        send, held = down(
-            parts, down_v, d_cols, right, shifts, z_count, hid_count, mem_local, scale_out
-        )
+        send, held = down(parts, down_v, d_cols, right, shifts, hid_count, mem_local, scale_out)
         held = held + along(send, core_pairs).astype(F32)
         half = held.shape[0] // 2
         held = held[half:] + along(held[:half].astype(BF16), x_pairs).astype(F32)
@@ -635,7 +625,7 @@
 
 
 def GROUPS(z_count):
-    return [(1,), *[tuple(range(z_count))[i : i + 2] for i in range(2, z_count, 2)], (0,)]
+    return [(1,), (0,), *[tuple(range(z_count))[i : i + 2] for i in range(2, z_count, 2)]]
 
 
 def solution(mesh):

time: 117 us -> 119 us (1.017)
  waiting for transfers between devices: 41.5 us -> 43.9 us
    ppermute x31, waiting for transfers between devices: 29.1 us -> 34.5 us  [along(): return lax.ppermute(v, 'pop', pairs)]
    ppermute x3, waiting for transfers between devices: 10.5 us -> 7.49 us  [local(): lax.ppermute(v, 'hid', [(i, (i + s + 1) % hid_count) for i in range(hid_c...]
where the time goes in v1:
time: 119 us
  waiting for transfers between devices  43.9 us (37%)
  Pallas kernels  36.6 us (31%)
  starting transfers between devices  36.3 us (31%)
    ppermute x31, waiting for transfers between devices, along(): return lax.ppermute(v, 'pop', pairs)  34.5 us
    ppermute x31, starting transfers between devices, along(): return lax.ppermute(v, 'pop', pairs)  27.8 us
    pallas_call x2, Pallas kernels, input_step(): pl.pallas_call(functools.partial(input_step_kernel, index, group, factor)...  8.42 us
    pallas_call x3, Pallas kernels, gate_up(): pl.pallas_call(functools.partial(gate_up_kernel, shifts, hid_count, rows...  7.54 us
    ppermute x3, waiting for transfers between devices, local(): lax.ppermute(v, 'hid', [(i, (i + s + 1) % hid_count) for i in range(hid_c...  7.49 us
    ppermute x3, starting transfers between devices, local(): lax.ppermute(mine, 'hid', [((i + s) % hid_count, i) for i in range(hid_co...  4.75 us
    pallas_call x3, Pallas kernels, down(): pl.pallas_call(functools.partial(down_kernel, shifts, hid_count, mem_loca...  4.43 us
    pallas_call x1, Pallas kernels, down_step(): pl.pallas_call(functools.partial(down_step_kernel, factor), grid=(hidden...  4.16 us
  transfers between devices with their start and end apart: 37, of which 12 were waited for; matrix products, arithmetic and copies ran while one was open for 0% of the time, Pallas kernels for 31%

profile of v1, /device:TPU:0, one launch (start us, length us, event | category | flops | bytes accessed | tf_op | source)
XLA Modules:
  0.0 118.8 jit_solution(14674010631521706081)
XLA Ops:
  0.6 3.0 %collective-permute-start.16 = (bf16[32,2048]{1,0:T(8,128)(2,1)}, bf16[32,2048]{1,0:T(8,128)(2,1)S(1)}, u32[]{:S(2)}, u32[]{:S(2)}) collective-permute-start(bf16[32,2048]{1,0:T(8,128)(2,1)} %refs_0_.1), channel_id=1, source_target_pairs={{0,4},{2,6},{4,0},{6,2},{8,12},{10,14},{12,8},{14,10},{16,20},{18,... | collective-permute-start | bytes 393224 | tf_op jit(solution)/shard_map/ppermute | solution.py:569
  3.7 1.3 %pack.1 = (bf16[4,24,1024]{2,1,0:T(8,128)(2,1)S(1)}, bf16[4,24,1024]{2,1,0:T(8,128)(2,1)S(1)}, bf16[4,24,1024]{2,1,0:T(8,128)(2,1)S(1)}, bf16[4,24,1024]{2,1,0:T(8,128)(2,1)S(1)}) custom-call(bf16[2,4,16384]{2,1,0:T(4,128)(2,1)} %gate_in.1, bf16[2,4,16384]{2,1,0:T(4,128)(2,1)} %up_in.1, bf16[2,4,16384]{2,1,0:T(4,128)(2,1)} %down_in.1), custom_call_target="tpu_custom_call" | custom-call | flops 67108864 | bytes 1572864 | tf_op jit(solution)/shard_map/pack/pallas_call | solution.py:94
  5.6 2.8 %collective-permute-start.23 = (bf16[32,2048]{1,0:T(8,128)(2,1)}, bf16[32,2048]{1,0:T(8,128)(2,1)S(1)}, u32[]{:S(2)}, u32[]{:S(2)}) collective-permute-start(bf16[32,2048]{1,0:T(8,128)(2,1)} %refs_0_.1), channel_id=1, source_target_pairs={{0,16},{2,18},{4,20},{6,22},{8,24},{10,26},{12,28},{14,30},{16,0},... | collective-permute-start | bytes 393224 | tf_op jit(solution)/shard_map/ppermute | solution.py:569
  8.4 2.8 %collective-permute-start.27 = (bf16[32,2048]{1,0:T(8,128)(2,1)}, bf16[32,2048]{1,0:T(8,128)(2,1)S(1)}, u32[]{:S(2)}, u32[]{:S(2)}) collective-permute-start(bf16[32,2048]{1,0:T(8,128)(2,1)} %refs_0_.1), channel_id=1, source_target_pairs={{0,24},{2,26},{4,28},{6,30},{8,16},{10,18},{12,20},{14,22},{16,8},... | collective-permute-start | bytes 393224 | tf_op jit(solution)/shard_map/ppermute | solution.py:569
  11.2 7.6 %collective-permute-done.23.refs_0_ = bf16[32,2048]{1,0:T(8,128)(2,1)S(1)} collective-permute-done((bf16[32,2048]{1,0:T(8,128)(2,1)}, bf16[32,2048]{1,0:T(8,128)(2,1)S(1)}, u32[]{:S(2)}, u32[]{:S(2)}) %collective-permute-start.23) | collective-permute-done | bytes 131104 | tf_op jit(solution)/shard_map/ppermute | solution.py:569
  18.8 0.5 collective-permute-start.18
  19.3 0.7 collective-permute-done.refs_0_
  20.0 1.5 %collective-permute-start.24 = (bf16[32,2048]{1,0:T(8,128)(2,1)S(1)}, bf16[32,2048]{1,0:T(8,128)(2,1)S(1)}, u32[]{:S(2)}, u32[]{:S(2)}) collective-permute-start(bf16[32,2048]{1,0:T(8,128)(2,1)S(1)} %collective-permute-done.23.refs_0_), channel_id=1, source_target_pairs={{0,4},{2,6},{4,0},{6,2},{8,12},{10,14},{12,8},{14,10},{16,20},{18,... | collective-permute-start | bytes 393224 | tf_op jit(solution)/shard_map/ppermute | solution.py:569
  22.0 1.5 %collective-permute-start.8 = (bf16[4,24,1024]{2,1,0:T(8,128)(2,1)S(1)}, bf16[4,24,1024]{2,1,0:T(8,128)(2,1)S(1)}, u32[]{:S(2)}, u32[]{:S(2)}) collective-permute-start(bf16[4,24,1024]{2,1,0:T(8,128)(2,1)S(1)} %collective-permute-done.7), channel_id=1, source_target_pairs={{0,4},{2,6},{4,0},{6,2},{8,12},{10,14},{12,8},{14,10},{16,20},{18,... | collective-permute-start | bytes 589832 | tf_op jit(solution)/shard_map/ppermute | solution.py:569
  23.6 3.8 %load.1 = (bf16[256,2048]{1,0:T(8,128)(2,1)S(1)}, bf16[2048,1024]{1,0:T(8,128)(2,1)S(1)}, bf16[2048,1024]{1,0:T(8,128)(2,1)S(1)}) custom-call(bf16[32,4,2048]{2,1,0:T(4,128)(2,1)} %gif_in.3, bf16[32,4,2048]{2,1,0:T(4,128)(2,1)} %uif_in.3, bf16[2048,1024]{1,0:T(8,128)(2,1)} %gw_in.1, bf16[2048,1024]{1,0:T(8,128)(2,1)} %uw_in.1), custom_call_target="tpu_custom_call" | custom-call | flops 2147483648 | bytes 8388608 | tf_op jit(solution)/shard_map/load/pallas_call | solution.py:156
  27.5 0.5 collective-permute-start.29
  28.5 0.7 collective-permute-done.28.refs_5_
  29.2 3.8 %collective-permute-done.8.refs_3_ = bf16[4,24,1024]{2,1,0:T(8,128)(2,1)S(1)} collective-permute-done((bf16[4,24,1024]{2,1,0:T(8,128)(2,1)S(1)}, bf16[4,24,1024]{2,1,0:T(8,128)(2,1)S(1)}, u32[]{:S(2)}, u32[]{:S(2)}) %collective-permute-start.8) | collective-permute-done | bytes 196640 | tf_op jit(solution)/shard_map/ppermute | solution.py:569
  32.9 2.3 %turn.1.in_ref = bf16[2048,256]{1,0:T(8,128)(2,1)S(1)} custom-call(s32[32]{0:T(128)S(1)} %copy-done.1, bf16[32,4,2048]{2,1,0:T(4,128)(2,1)} %gif_in.3, bf16[32,4,2048]{2,1,0:T(4,128)(2,1)} %uif_in.3), custom_call_target="tpu_custom_call" | custom-call | flops 1073741824 | bytes 2097152 | tf_op jit(solution)/shard_map/turn/pallas_call | solution.py:204
  35.3 2.2 %gate_up.4 = (bf16[64,2176]{1,0:T(8,128)(2,1)S(1)}, f32[64,2048]{1,0:T(8,128)S(1)}, bf16[64,128]{1,0:T(8,128)(2,1)S(1)}) custom-call(bf16[32,2048]{1,0:T(8,128)(2,1)S(1)} %copy-done, bf16[32,2048]{1,0:T(8,128)(2,1)S(1)} %collective-permute-done.16.refs_1_, bf16[32,2048]{1,0:T(8,128)(2,1)S(1)} %collective-permute-done.17.refs_2_, ...), custom_call_target="tpu_custom_call" | custom-call | flops 1073741824 | bytes 8388608 | tf_op jit(solution)/shard_map/gate_up/pallas_call | solution.py:351
  37.6 0.6 collective-permute-start.2
  38.3 2.4 %collective-permute-start.9 = (bf16[96,1024]{1,0:T(8,128)(2,1)S(1)}, bf16[96,1024]{1,0:T(8,128)(2,1)S(1)}, u32[]{:S(2)}, u32[]{:S(2)}) collective-permute-start(bf16[96,1024]{1,0:T(8,128)(2,1)S(1)} %get-tuple-element.47), channel_id=1, source_target_pairs={{0,8},{2,10},{4,12},{6,14},{8,0},{10,2},{12,4},{14,6},{16,24},{18,... | collective-permute-start | bytes 589832 | tf_op jit(solution)/shard_map/ppermute | solution.py:569
  40.7 1.9 %collective-permute-start.10 = (bf16[96,1024]{1,0:T(8,128)(2,1)S(1)}, bf16[96,1024]{1,0:T(8,128)(2,1)S(1)}, u32[]{:S(2)}, u32[]{:S(2)}) collective-permute-start(bf16[96,1024]{1,0:T(8,128)(2,1)S(1)} %get-tuple-element.48), channel_id=1, source_target_pairs={{0,16},{2,18},{4,20},{6,22},{8,24},{10,26},{12,28},{14,30},{16,0},... | collective-permute-start | bytes 589832 | tf_op jit(solution)/shard_map/ppermute | solution.py:569
  42.6 1.5 %collective-permute-start.11 = (bf16[96,1024]{1,0:T(8,128)(2,1)S(1)}, bf16[96,1024]{1,0:T(8,128)(2,1)S(1)}, u32[]{:S(2)}, u32[]{:S(2)}) collective-permute-start(bf16[96,1024]{1,0:T(8,128)(2,1)S(1)} %get-tuple-element.49), channel_id=1, source_target_pairs={{0,24},{2,26},{4,28},{6,30},{8,16},{10,18},{12,20},{14,22},{16,8},... | collective-permute-start | bytes 589832 | tf_op jit(solution)/shard_map/ppermute | solution.py:569
  44.0 3.1 %gate_up.5 = (bf16[128,2176]{1,0:T(8,128)(2,1)S(1)}, f32[128,2048]{1,0:T(8,128)S(1)}, bf16[128,128]{1,0:T(8,128)(2,1)S(1)}) custom-call(bf16[32,2048]{1,0:T(8,128)(2,1)S(1)} %collective-permute-done.23.refs_0_, bf16[32,2048]{1,0:T(8,128)(2,1)S(1)} %collective-permute-done.24.refs_1_, bf16[32,2048]{1,0:T(8,128)(2,1)S(1)} %collective-permute-done.25.refs_2_, ...), custom_call_target="tpu_custom_call" | custom-call | flops 2147483648 | bytes 8388608 | tf_op jit(solution)/shard_map/gate_up/pallas_call | solution.py:351
  47.1 1.6 %collective-permute-start.19 = (bf16[64,2176]{1,0:T(8,128)(2,1)S(1)}, bf16[64,2176]{1,0:T(8,128)(2,1)S(1)}, u32[]{:S(2)}, u32[]{:S(2)}) collective-permute-start(bf16[64,2176]{1,0:T(8,128)(2,1)S(1)} %get-tuple-element.58), channel_id=1, source_target_pairs={{0,1},{1,0},{2,3},{3,2},{4,5},{5,4},{6,7},{7,6},{8,9},{9,8},{10,11... | collective-permute-start | bytes 835592 | tf_op jit(solution)/shard_map/ppermute | solution.py:601
  48.7 0.5 collective-permute-start.31
  49.2 2.2 %gate_up.3 = (bf16[64,2176]{1,0:T(8,128)(2,1)S(1)}, f32[64,2048]{1,0:T(8,128)S(1)}, bf16[64,128]{1,0:T(8,128)(2,1)S(1)}) custom-call(bf16[32,2048]{1,0:T(8,128)(2,1)S(1)} %collective-permute-done.refs_0_, bf16[32,2048]{1,0:T(8,128)(2,1)S(1)} %collective-permute-done.1.refs_1_, bf16[32,2048]{1,0:T(8,128)(2,1)S(1)} %collective-permute-done.2.refs_2_, ...), custom_call_target="tpu_custom_call" | custom-call | flops 1073741824 | bytes 8388608 | tf_op jit(solution)/shard_map/gate_up/pallas_call | solution.py:351
  51.4 1.6 %collective-permute-start.4 = (bf16[64,2176]{1,0:T(8,128)(2,1)S(1)}, bf16[64,2176]{1,0:T(8,128)(2,1)S(1)}, u32[]{:S(2)}, u32[]{:S(2)}) collective-permute-start(bf16[64,2176]{1,0:T(8,128)(2,1)S(1)} %get-tuple-element.41), channel_id=1, source_target_pairs={{0,1},{1,0},{2,3},{3,2},{4,5},{5,4},{6,7},{7,6},{8,9},{9,8},{10,11... | collective-permute-start | bytes 835592 | tf_op jit(solution)/shard_map/ppermute | solution.py:601
  53.0 4.8 %collective-permute-done.10.refs_2_ = bf16[96,1024]{1,0:T(8,128)(2,1)S(1)} collective-permute-done((bf16[96,1024]{1,0:T(8,128)(2,1)S(1)}, bf16[96,1024]{1,0:T(8,128)(2,1)S(1)}, u32[]{:S(2)}, u32[]{:S(2)}) %collective-permute-start.10) | collective-permute-done | bytes 196640 | tf_op jit(solution)/shard_map/ppermute | solution.py:569
  57.8 3.0 %arrange.1 = (bf16[256,1024]{1,0:T(8,128)(2,1)S(1)}, bf16[128,1024]{1,0:T(8,128)(2,1)S(1)}, bf16[1024,128]{1,0:T(8,128)(2,1)S(1)}, bf16[128,2048]{1,0:T(8,128)(2...) custom-call(s32[32]{0:T(128)S(1)} %copy-done.1, bf16[32,4,2048]{2,1,0:T(4,128)(2,1)} %right_in.1, ...), custom_call_target="tpu_custom_call" | custom-call | flops 2147483648 | bytes 8388608 | tf_op jit(solution)/shard_map/arrange/pallas_call | solution.py:248
  61.3 1.6 %collective-permute-start.20 = (bf16[64,1024]{1,0:T(8,128)(2,1)S(1)}, bf16[64,1024]{1,0:T(8,128)(2,1)S(1)}, u32[]{:S(2)}, u32[]{:S(2)}) collective-permute-start(bf16[64,1024]{1,0:T(8,128)(2,1)S(1)} %make_hidden.4.refs_0_), channel_id=1, source_target_pairs={{1,0},{0,1},{3,2},{2,3},{5,4},{4,5},{7,6},{6,7},{9,8},{8,9},{11,10... | collective-permute-start | bytes 393224 | tf_op jit(solution)/shard_map/ppermute | solution.py:606
  62.9 4.2 %shard_map.138 = f32[2048,1024]{1,0:T(8,128)} custom-call(bf16[2048,256]{1,0:T(8,128)(2,1)S(1)} %turn.1.in_ref, bf16[256,1024]{1,0:T(8,128)(2,1)S(1)} %get-tuple-element.50.refs_3_.cols_ref), custom_call_target="tpu_custom_call" | custom-call | flops 4294967296 | bytes 8388608 | tf_op jit(solution)/shard_map/pallas_call | solution.py:500
  67.1 7.5 %collective-permute-done.4.refs_2_ = bf16[64,2176]{1,0:T(8,128)(2,1)S(1)} collective-permute-done((bf16[64,2176]{1,0:T(8,128)(2,1)S(1)}, bf16[64,2176]{1,0:T(8,128)(2,1)S(1)}, u32[]{:S(2)}, u32[]{:S(2)}) %collective-permute-start.4) | collective-permute-done | bytes 278560 | tf_op jit(solution)/shard_map/ppermute | solution.py:601
  75.1 1.6 %collective-permute-start.12 = (bf16[64,1024]{1,0:T(8,128)(2,1)S(1)}, bf16[64,1024]{1,0:T(8,128)(2,1)S(1)}, u32[]{:S(2)}, u32[]{:S(2)}) collective-permute-start(bf16[64,1024]{1,0:T(8,128)(2,1)S(1)} %make_hidden.3.refs_0_), channel_id=1, source_target_pairs={{1,0},{0,1},{3,2},{2,3},{5,4},{4,5},{7,6},{6,7},{9,8},{8,9},{11,10... | collective-permute-start | bytes 393224 | tf_op jit(solution)/shard_map/ppermute | solution.py:606
  77.0 1.2 %down.4 = (bf16[64,2048]{1,0:T(8,128)(2,1)S(1)}, f32[64,2048]{1,0:T(8,128)S(1)}) custom-call(bf16[64,1024]{1,0:T(8,128)(2,1)S(1)} %make_hidden.4.refs_0_, bf16[64,1024]{1,0:T(8,128)(2,1)S(1)} %collective-permute-done.20.refs_1_, bf16[1024,2048]{1,0:T(8,128)(2,1)S(1)} %get-tuple-element.51.refs_2_, bf16[128,1024]{1,0:T(8,128)(2,1)S(1)} %get-tuple-element.52.refs_3_, ...), custom_call_target="tpu_custom_call" | custom-call | flops 536870912 | bytes 4194304 | tf_op jit(solution)/shard_map/down/pallas_call | solution.py:471
  78.3 0.6 make_hidden.5.refs_0_
  78.9 1.6 %collective-permute-start.32 = (bf16[128,1024]{1,0:T(8,128)(2,1)S(1)}, bf16[128,1024]{1,0:T(8,128)(2,1)S(1)}, u32[]{:S(2)}, u32[]{:S(2)}) collective-permute-start(bf16[128,1024]{1,0:T(8,128)(2,1)S(1)} %make_hidden.5.refs_0_), channel_id=1, source_target_pairs={{1,0},{0,1},{3,2},{2,3},{5,4},{4,5},{7,6},{6,7},{9,8},{8,9},{11,10... | collective-permute-start | bytes 786440 | tf_op jit(solution)/shard_map/ppermute | solution.py:606
  80.5 4.2 %shard_map.139 = f32[2048,1024]{1,0:T(8,128)} custom-call(bf16[2048,256]{1,0:T(8,128)(2,1)S(1)} %turn.1.in_ref, bf16[256,1024]{1,0:T(8,128)(2,1)S(1)} %get-tuple-element.50.refs_3_.cols_ref), custom_call_target="tpu_custom_call" | custom-call | flops 4294967296 | bytes 8388608 | tf_op jit(solution)/shard_map/pallas_call | solution.py:500
  84.7 1.2 %down.3 = (bf16[64,2048]{1,0:T(8,128)(2,1)S(1)}, f32[64,2048]{1,0:T(8,128)S(1)}) custom-call(bf16[64,1024]{1,0:T(8,128)(2,1)S(1)} %make_hidden.3.refs_0_, bf16[64,1024]{1,0:T(8,128)(2,1)S(1)} %collective-permute-done.12.refs_1_, bf16[1024,2048]{1,0:T(8,128)(2,1)S(1)} %get-tuple-element.51.refs_2_, bf16[128,1024]{1,0:T(8,128)(2,1)S(1)} %get-tuple-element.52.refs_3_, ...), custom_call_target="tpu_custom_call" | custom-call | flops 536870912 | bytes 4194304 | tf_op jit(solution)/shard_map/down/pallas_call | solution.py:471
  86.2 1.5 %collective-permute-done.32.refs_1_ = bf16[128,1024]{1,0:T(8,128)(2,1)S(1)} collective-permute-done((bf16[128,1024]{1,0:T(8,128)(2,1)S(1)}, bf16[128,1024]{1,0:T(8,128)(2,1)S(1)}, u32[]{:S(2)}, u32[]{:S(2)}) %collective-permute-start.32) | collective-permute-done | bytes 262176 | tf_op jit(solution)/shard_map/ppermute | solution.py:606
  87.7 2.1 %down.5 = (bf16[128,2048]{1,0:T(8,128)(2,1)S(1)}, f32[128,2048]{1,0:T(8,128)S(1)}) custom-call(bf16[128,1024]{1,0:T(8,128)(2,1)S(1)} %make_hidden.5.refs_0_, bf16[128,1024]{1,0:T(8,128)(2,1)S(1)} %collective-permute-done.32.refs_1_, bf16[1024,2048]{1,0:T(8,128)(2,1)S(1)} %get-tuple-element.51.refs_2_, bf16[128,1024]{1,0:T(8,128)(2,1)S(1)} %get-tuple-element.52.refs_3_, ...), custom_call_target="tpu_custom_call" | custom-call | flops 1073741824 | bytes 4194304 | tf_op jit(solution)/shard_map/down/pallas_call | solution.py:471
  89.9 1.5 %collective-permute-start.22 = (bf16[32,2048]{1,0:T(8,128)(2,1)S(1)}, bf16[32,2048]{1,0:T(8,128)(2,1)S(1)}, u32[]{:S(2)}, u32[]{:S(2)}) collective-permute-start(bf16[32,2048]{1,0:T(8,128)(2,1)S(1)} %slice.64), channel_id=1, source_target_pairs={{0,4},{2,6},{4,0},{6,2},{8,12},{10,14},{12,8},{14,10},{16,20},{18,... | collective-permute-start | bytes 393224 | tf_op jit(solution)/shard_map/ppermute | solution.py:569
  91.5 0.6 collective-permute-start.14
  92.3 1.5 %collective-permute-start.34 = (bf16[64,2048]{1,0:T(8,128)(2,1)S(1)}, bf16[64,2048]{1,0:T(8,128)(2,1)S(1)}, u32[]{:S(2)}, u32[]{:S(2)}) collective-permute-start(bf16[64,2048]{1,0:T(8,128)(2,1)S(1)} %slice.63), channel_id=1, source_target_pairs={{0,4},{2,6},{4,0},{6,2},{8,12},{10,14},{12,8},{14,10},{16,20},{18,... | collective-permute-start | bytes 786440 | tf_op jit(solution)/shard_map/ppermute | solution.py:569
  93.9 5.3 %collective-permute-done.14 = bf16[32,2048]{1,0:T(8,128)(2,1)S(1)} collective-permute-done((bf16[32,2048]{1,0:T(8,128)(2,1)S(1)}, bf16[32,2048]{1,0:T(8,128)(2,1)S(1)}, u32[]{:S(2)}, u32[]{:S(2)}) %collective-permute-start.14) | collective-permute-done | bytes 131104 | tf_op jit(solution)/shard_map/ppermute | solution.py:569
  99.2 0.6 collective-permute-start.15
  99.7 4.6 %collective-permute-done.34 = bf16[64,2048]{1,0:T(8,128)(2,1)S(1)} collective-permute-done((bf16[64,2048]{1,0:T(8,128)(2,1)S(1)}, bf16[64,2048]{1,0:T(8,128)(2,1)S(1)}, u32[]{:S(2)}, u32[]{:S(2)}) %collective-permute-start.34) | collective-permute-done | bytes 262176 | tf_op jit(solution)/shard_map/ppermute | solution.py:569
  104.4 2.4 %collective-permute-start.36 = (bf16[32,2048]{1,0:T(8,128)(2,1)S(1)}, bf16[32,2048]{1,0:T(8,128)(2,1)S(1)}, u32[]{:S(2)}, u32[]{:S(2)}) collective-permute-start(bf16[32,2048]{1,0:T(8,128)(2,1)S(1)} %get-tuple-element.69), channel_id=1, source_target_pairs={{0,24},{2,26},{4,28},{6,30},{8,16},{10,18},{12,20},{14,22},{16,8},... | collective-permute-start | bytes 393224 | tf_op jit(solution)/shard_map/ppermute | solution.py:569
  106.8 4.2 %down_step.1 = f32[1024,2048]{1,0:T(8,128)} custom-call(bf16[1024,128]{1,0:T(8,128)(2,1)S(1)} %get-tuple-element.66.left_ref, bf16[128,2048]{1,0:T(8,128)(2,1)S(1)} %get-tuple-element.67.right_ref), custom_call_target="tpu_custom_call" | custom-call | flops 2147483648 | bytes 8388608 | tf_op jit(solution)/shard_map/down_step/pallas_call | solution.py:523
  111.0 1.7 %collective-permute-done.36 = bf16[32,2048]{1,0:T(8,128)(2,1)S(1)} collective-permute-done((bf16[32,2048]{1,0:T(8,128)(2,1)S(1)}, bf16[32,2048]{1,0:T(8,128)(2,1)S(1)}, u32[]{:S(2)}, u32[]{:S(2)}) %collective-permute-start.36) | collective-permute-done | bytes 131104 | tf_op jit(solution)/shard_map/ppermute | solution.py:569
  112.6 5.4 %collective-permute-done.35 = bf16[32,2048]{1,0:T(8,128)(2,1)S(1)} collective-permute-done((bf16[32,2048]{1,0:T(8,128)(2,1)S(1)}, bf16[32,2048]{1,0:T(8,128)(2,1)S(1)}, u32[]{:S(2)}, u32[]{:S(2)}) %collective-permute-start.35) | collective-permute-done | bytes 131104 | tf_op jit(solution)/shard_map/ppermute | solution.py:569
  118.1 0.7 fusion.4
  (57 shorter events, 4.0 us)
Async XLA Ops:
  0.6 7.8 %collective-permute-start.16 = (bf16[32,2048]{1,0:T(8,128)(2,1)}, bf16[32,2048]{1,0:T(8,128)(2,1)S(1)}, u32[]{:S(2)}, u32[]{:S(2)}) collective-permute-start(bf16[32,2048]{1,0:T(8,128)(2,1)} %refs_0_.1), channel_id=1, source_target_pairs={{0,4},{2,6},{4,0},{6,2},{8,12},{10,14},{12,8},{14,10},{16,20},{18,... | collective-permute-start | bytes 393224 | tf_op jit(solution)/shard_map/ppermute | solution.py:569
  3.7 7.6 %collective-permute-start.17 = (bf16[32,2048]{1,0:T(8,128)(2,1)}, bf16[32,2048]{1,0:T(8,128)(2,1)S(1)}, u32[]{:S(2)}, u32[]{:S(2)}) collective-permute-start(bf16[32,2048]{1,0:T(8,128)(2,1)} %refs_0_.1), channel_id=1, source_target_pairs={{0,2},{2,0},{4,6},{6,4},{8,10},{10,8},{12,14},{14,12},{16,18},{18,... | collective-permute-start | bytes 393224 | tf_op jit(solution)/shard_map/ppermute | solution.py:569
  5.0 16.6 %collective-permute-start.5 = (bf16[4,24,1024]{2,1,0:T(8,128)(2,1)S(1)}, bf16[4,24,1024]{2,1,0:T(8,128)(2,1)S(1)}, u32[]{:S(2)}, u32[]{:S(2)}) collective-permute-start(bf16[4,24,1024]{2,1,0:T(8,128)(2,1)S(1)} %get-tuple-element.43), channel_id=1, source_target_pairs={{0,4},{2,6},{4,0},{6,2},{8,12},{10,14},{12,8},{14,10},{16,20},{18,... | collective-permute-start | bytes 589832 | tf_op jit(solution)/shard_map/ppermute | solution.py:569
  5.1 16.9 %collective-permute-start.7 = (bf16[4,24,1024]{2,1,0:T(8,128)(2,1)S(1)}, bf16[4,24,1024]{2,1,0:T(8,128)(2,1)S(1)}, u32[]{:S(2)}, u32[]{:S(2)}) collective-permute-start(bf16[4,24,1024]{2,1,0:T(8,128)(2,1)S(1)} %get-tuple-element.45), channel_id=1, source_target_pairs={{0,2},{2,0},{4,6},{6,4},{8,10},{10,8},{12,14},{14,12},{16,18},{18,... | collective-permute-start | bytes 589832 | tf_op jit(solution)/shard_map/ppermute | solution.py:569
  5.6 13.1 %collective-permute-start.23 = (bf16[32,2048]{1,0:T(8,128)(2,1)}, bf16[32,2048]{1,0:T(8,128)(2,1)S(1)}, u32[]{:S(2)}, u32[]{:S(2)}) collective-permute-start(bf16[32,2048]{1,0:T(8,128)(2,1)} %refs_0_.1), channel_id=1, source_target_pairs={{0,16},{2,18},{4,20},{6,22},{8,24},{10,26},{12,28},{14,30},{16,0},... | collective-permute-start | bytes 393224 | tf_op jit(solution)/shard_map/ppermute | solution.py:569
  8.4 10.4 %collective-permute-start.27 = (bf16[32,2048]{1,0:T(8,128)(2,1)}, bf16[32,2048]{1,0:T(8,128)(2,1)S(1)}, u32[]{:S(2)}, u32[]{:S(2)}) collective-permute-start(bf16[32,2048]{1,0:T(8,128)(2,1)} %refs_0_.1), channel_id=1, source_target_pairs={{0,24},{2,26},{4,28},{6,30},{8,16},{10,18},{12,20},{14,22},{16,8},... | collective-permute-start | bytes 393224 | tf_op jit(solution)/shard_map/ppermute | solution.py:569
  11.2 8.8 %collective-permute-start = (bf16[32,2048]{1,0:T(8,128)(2,1)}, bf16[32,2048]{1,0:T(8,128)(2,1)S(1)}, u32[]{:S(2)}, u32[]{:S(2)}) collective-permute-start(bf16[32,2048]{1,0:T(8,128)(2,1)} %refs_0_.1), channel_id=1, source_target_pairs={{0,8},{2,10},{4,12},{6,14},{8,0},{10,2},{12,4},{14,6},{16,24},{18,... | collective-permute-start | bytes 393224 | tf_op jit(solution)/shard_map/ppermute | solution.py:569
  18.8 14.2 %copy-start.1 = (s32[32]{0:T(128)S(1)}, s32[32]{0:T(128)}, u32[]{:S(2)}) copy-start(s32[32]{0:T(128)} %ranks_ref.3) | copy-start | bytes 388
  18.8 16.5 %copy-start = (bf16[32,2048]{1,0:T(8,128)(2,1)S(1)}, bf16[32,2048]{1,0:T(8,128)(2,1)}, u32[]{:S(2)}) copy-start(bf16[32,2048]{1,0:T(8,128)(2,1)} %refs_0_.1) | copy-start | bytes 393220
  18.8 8.6 %collective-permute-start.6 = (bf16[4,24,1024]{2,1,0:T(8,128)(2,1)S(1)}, bf16[4,24,1024]{2,1,0:T(8,128)(2,1)S(1)}, u32[]{:S(2)}, u32[]{:S(2)}) collective-permute-start(bf16[4,24,1024]{2,1,0:T(8,128)(2,1)S(1)} %get-tuple-element.44), channel_id=1, source_target_pairs={{0,2},{2,0},{4,6},{6,4},{8,10},{10,8},{12,14},{14,12},{16,18},{18,... | collective-permute-start | bytes 589832 | tf_op jit(solution)/shard_map/ppermute | solution.py:569
  18.8 8.7 %collective-permute-start.18 = (bf16[32,2048]{1,0:T(8,128)(2,1)S(1)}, bf16[32,2048]{1,0:T(8,128)(2,1)S(1)}, u32[]{:S(2)}, u32[]{:S(2)}) collective-permute-start(bf16[32,2048]{1,0:T(8,128)(2,1)S(1)} %collective-permute-done.16.refs_1_), channel_id=1, source_target_pairs={{0,2},{2,0},{4,6},{6,4},{8,10},{10,8},{12,14},{14,12},{16,18},{18,... | collective-permute-start | bytes 393224 | tf_op jit(solution)/shard_map/ppermute | solution.py:569
  20.0 8.0 %collective-permute-start.24 = (bf16[32,2048]{1,0:T(8,128)(2,1)S(1)}, bf16[32,2048]{1,0:T(8,128)(2,1)S(1)}, u32[]{:S(2)}, u32[]{:S(2)}) collective-permute-start(bf16[32,2048]{1,0:T(8,128)(2,1)S(1)} %collective-permute-done.23.refs_0_), channel_id=1, source_target_pairs={{0,4},{2,6},{4,0},{6,2},{8,12},{10,14},{12,8},{14,10},{16,20},{18,... | collective-permute-start | bytes 393224 | tf_op jit(solution)/shard_map/ppermute | solution.py:569
  21.5 7.6 %collective-permute-start.28 = (bf16[32,2048]{1,0:T(8,128)(2,1)S(1)}, bf16[32,2048]{1,0:T(8,128)(2,1)S(1)}, u32[]{:S(2)}, u32[]{:S(2)}) collective-permute-start(bf16[32,2048]{1,0:T(8,128)(2,1)S(1)} %collective-permute-done.27.refs_4_), channel_id=1, source_target_pairs={{0,4},{2,6},{4,0},{6,2},{8,12},{10,14},{12,8},{14,10},{16,20},{18,... | collective-permute-start | bytes 393224 | tf_op jit(solution)/shard_map/ppermute | solution.py:569
  22.0 10.9 %collective-permute-start.8 = (bf16[4,24,1024]{2,1,0:T(8,128)(2,1)S(1)}, bf16[4,24,1024]{2,1,0:T(8,128)(2,1)S(1)}, u32[]{:S(2)}, u32[]{:S(2)}) collective-permute-start(bf16[4,24,1024]{2,1,0:T(8,128)(2,1)S(1)} %collective-permute-done.7), channel_id=1, source_target_pairs={{0,4},{2,6},{4,0},{6,2},{8,12},{10,14},{12,8},{14,10},{16,20},{18,... | collective-permute-start | bytes 589832 | tf_op jit(solution)/shard_map/ppermute | solution.py:569
  27.4 10.2 %collective-permute-start.25 = (bf16[32,2048]{1,0:T(8,128)(2,1)S(1)}, bf16[32,2048]{1,0:T(8,128)(2,1)S(1)}, u32[]{:S(2)}, u32[]{:S(2)}) collective-permute-start(bf16[32,2048]{1,0:T(8,128)(2,1)S(1)} %collective-permute-done.23.refs_0_), channel_id=1, source_target_pairs={{0,2},{2,0},{4,6},{6,4},{8,10},{10,8},{12,14},{14,12},{16,18},{18,... | collective-permute-start | bytes 393224 | tf_op jit(solution)/shard_map/ppermute | solution.py:569
  27.5 10.8 %collective-permute-start.29 = (bf16[32,2048]{1,0:T(8,128)(2,1)S(1)}, bf16[32,2048]{1,0:T(8,128)(2,1)S(1)}, u32[]{:S(2)}, u32[]{:S(2)}) collective-permute-start(bf16[32,2048]{1,0:T(8,128)(2,1)S(1)} %collective-permute-done.27.refs_4_), channel_id=1, source_target_pairs={{0,2},{2,0},{4,6},{6,4},{8,10},{10,8},{12,14},{14,12},{16,18},{18,... | collective-permute-start | bytes 393224 | tf_op jit(solution)/shard_map/ppermute | solution.py:569
  28.0 10.2 %collective-permute-start.1 = (bf16[32,2048]{1,0:T(8,128)(2,1)S(1)}, bf16[32,2048]{1,0:T(8,128)(2,1)S(1)}, u32[]{:S(2)}, u32[]{:S(2)}) collective-permute-start(bf16[32,2048]{1,0:T(8,128)(2,1)S(1)} %collective-permute-done.refs_0_), channel_id=1, source_target_pairs={{0,4},{2,6},{4,0},{6,2},{8,12},{10,14},{12,8},{14,10},{16,20},{18,... | collective-permute-start | bytes 393224 | tf_op jit(solution)/shard_map/ppermute | solution.py:569
  29.2 11.5 %collective-permute-start.26 = (bf16[32,2048]{1,0:T(8,128)(2,1)S(1)}, bf16[32,2048]{1,0:T(8,128)(2,1)S(1)}, u32[]{:S(2)}, u32[]{:S(2)}) collective-permute-start(bf16[32,2048]{1,0:T(8,128)(2,1)S(1)} %collective-permute-done.24.refs_1_), channel_id=1, source_target_pairs={{0,2},{2,0},{4,6},{6,4},{8,10},{10,8},{12,14},{14,12},{16,18},{18,... | collective-permute-start | bytes 393224 | tf_op jit(solution)/shard_map/ppermute | solution.py:569
  32.9 9.6 %collective-permute-start.30 = (bf16[32,2048]{1,0:T(8,128)(2,1)S(1)}, bf16[32,2048]{1,0:T(8,128)(2,1)S(1)}, u32[]{:S(2)}, u32[]{:S(2)}) collective-permute-start(bf16[32,2048]{1,0:T(8,128)(2,1)S(1)} %collective-permute-done.28.refs_5_), channel_id=1, source_target_pairs={{0,2},{2,0},{4,6},{6,4},{8,10},{10,8},{12,14},{14,12},{16,18},{18,... | collective-permute-start | bytes 393224 | tf_op jit(solution)/shard_map/ppermute | solution.py:569
  37.6 9.5 %collective-permute-start.2 = (bf16[32,2048]{1,0:T(8,128)(2,1)S(1)}, bf16[32,2048]{1,0:T(8,128)(2,1)S(1)}, u32[]{:S(2)}, u32[]{:S(2)}) collective-permute-start(bf16[32,2048]{1,0:T(8,128)(2,1)S(1)} %collective-permute-done.refs_0_), channel_id=1, source_target_pairs={{0,2},{2,0},{4,6},{6,4},{8,10},{10,8},{12,14},{14,12},{16,18},{18,... | collective-permute-start | bytes 393224 | tf_op jit(solution)/shard_map/ppermute | solution.py:569
  38.2 10.5 %collective-permute-start.3 = (bf16[32,2048]{1,0:T(8,128)(2,1)S(1)}, bf16[32,2048]{1,0:T(8,128)(2,1)S(1)}, u32[]{:S(2)}, u32[]{:S(2)}) collective-permute-start(bf16[32,2048]{1,0:T(8,128)(2,1)S(1)} %collective-permute-done.1.refs_1_), channel_id=1, source_target_pairs={{0,2},{2,0},{4,6},{6,4},{8,10},{10,8},{12,14},{14,12},{16,18},{18,... | collective-permute-start | bytes 393224 | tf_op jit(solution)/shard_map/ppermute | solution.py:569
  38.3 13.1 %collective-permute-start.9 = (bf16[96,1024]{1,0:T(8,128)(2,1)S(1)}, bf16[96,1024]{1,0:T(8,128)(2,1)S(1)}, u32[]{:S(2)}, u32[]{:S(2)}) collective-permute-start(bf16[96,1024]{1,0:T(8,128)(2,1)S(1)} %get-tuple-element.47), channel_id=1, source_target_pairs={{0,8},{2,10},{4,12},{6,14},{8,0},{10,2},{12,4},{14,6},{16,24},{18,... | collective-permute-start | bytes 589832 | tf_op jit(solution)/shard_map/ppermute | solution.py:569
  40.7 17.1 %collective-permute-start.10 = (bf16[96,1024]{1,0:T(8,128)(2,1)S(1)}, bf16[96,1024]{1,0:T(8,128)(2,1)S(1)}, u32[]{:S(2)}, u32[]{:S(2)}) collective-permute-start(bf16[96,1024]{1,0:T(8,128)(2,1)S(1)} %get-tuple-element.48), channel_id=1, source_target_pairs={{0,16},{2,18},{4,20},{6,22},{8,24},{10,26},{12,28},{14,30},{16,0},... | collective-permute-start | bytes 589832 | tf_op jit(solution)/shard_map/ppermute | solution.py:569
  42.6 15.3 %collective-permute-start.11 = (bf16[96,1024]{1,0:T(8,128)(2,1)S(1)}, bf16[96,1024]{1,0:T(8,128)(2,1)S(1)}, u32[]{:S(2)}, u32[]{:S(2)}) collective-permute-start(bf16[96,1024]{1,0:T(8,128)(2,1)S(1)} %get-tuple-element.49), channel_id=1, source_target_pairs={{0,24},{2,26},{4,28},{6,30},{8,16},{10,18},{12,20},{14,22},{16,8},... | collective-permute-start | bytes 589832 | tf_op jit(solution)/shard_map/ppermute | solution.py:569
  47.1 13.8 %collective-permute-start.19 = (bf16[64,2176]{1,0:T(8,128)(2,1)S(1)}, bf16[64,2176]{1,0:T(8,128)(2,1)S(1)}, u32[]{:S(2)}, u32[]{:S(2)}) collective-permute-start(bf16[64,2176]{1,0:T(8,128)(2,1)S(1)} %get-tuple-element.58), channel_id=1, source_target_pairs={{0,1},{1,0},{2,3},{3,2},{4,5},{5,4},{6,7},{7,6},{8,9},{9,8},{10,11... | collective-permute-start | bytes 835592 | tf_op jit(solution)/shard_map/ppermute | solution.py:601
  48.7 29.6 %collective-permute-start.31 = (bf16[128,2176]{1,0:T(8,128)(2,1)S(1)}, bf16[128,2176]{1,0:T(8,128)(2,1)S(1)}, u32[]{:S(2)}, u32[]{:S(2)}) collective-permute-start(bf16[128,2176]{1,0:T(8,128)(2,1)S(1)} %get-tuple-element.63), channel_id=1, source_target_pairs={{0,1},{1,0},{2,3},{3,2},{4,5},{5,4},{6,7},{7,6},{8,9},{9,8},{10,11... | collective-permute-start | bytes 1671176 | tf_op jit(solution)/shard_map/ppermute | solution.py:601
  51.4 23.2 %collective-permute-start.4 = (bf16[64,2176]{1,0:T(8,128)(2,1)S(1)}, bf16[64,2176]{1,0:T(8,128)(2,1)S(1)}, u32[]{:S(2)}, u32[]{:S(2)}) collective-permute-start(bf16[64,2176]{1,0:T(8,128)(2,1)S(1)} %get-tuple-element.41), channel_id=1, source_target_pairs={{0,1},{1,0},{2,3},{3,2},{4,5},{5,4},{6,7},{7,6},{8,9},{9,8},{10,11... | collective-permute-start | bytes 835592 | tf_op jit(solution)/shard_map/ppermute | solution.py:601
  61.3 15.7 %collective-permute-start.20 = (bf16[64,1024]{1,0:T(8,128)(2,1)S(1)}, bf16[64,1024]{1,0:T(8,128)(2,1)S(1)}, u32[]{:S(2)}, u32[]{:S(2)}) collective-permute-start(bf16[64,1024]{1,0:T(8,128)(2,1)S(1)} %make_hidden.4.refs_0_), channel_id=1, source_target_pairs={{1,0},{0,1},{3,2},{2,3},{5,4},{4,5},{7,6},{6,7},{9,8},{8,9},{11,10... | collective-permute-start | bytes 393224 | tf_op jit(solution)/shard_map/ppermute | solution.py:606
  75.1 9.6 %collective-permute-start.12 = (bf16[64,1024]{1,0:T(8,128)(2,1)S(1)}, bf16[64,1024]{1,0:T(8,128)(2,1)S(1)}, u32[]{:S(2)}, u32[]{:S(2)}) collective-permute-start(bf16[64,1024]{1,0:T(8,128)(2,1)S(1)} %make_hidden.3.refs_0_), channel_id=1, source_target_pairs={{1,0},{0,1},{3,2},{2,3},{5,4},{4,5},{7,6},{6,7},{9,8},{8,9},{11,10... | collective-permute-start | bytes 393224 | tf_op jit(solution)/shard_map/ppermute | solution.py:606
  78.2 11.6 %collective-permute-start.21 = (bf16[64,2048]{1,0:T(8,128)(2,1)S(1)}, bf16[64,2048]{1,0:T(8,128)(2,1)S(1)}, u32[]{:S(2)}, u32[]{:S(2)}) collective-permute-start(bf16[64,2048]{1,0:T(8,128)(2,1)S(1)} %get-tuple-element.60), channel_id=1, source_target_pairs={{0,2},{2,0},{4,6},{6,4},{8,10},{10,8},{12,14},{14,12},{16,18},{18,... | collective-permute-start | bytes 786440 | tf_op jit(solution)/shard_map/ppermute | solution.py:569
  78.9 8.8 %collective-permute-start.32 = (bf16[128,1024]{1,0:T(8,128)(2,1)S(1)}, bf16[128,1024]{1,0:T(8,128)(2,1)S(1)}, u32[]{:S(2)}, u32[]{:S(2)}) collective-permute-start(bf16[128,1024]{1,0:T(8,128)(2,1)S(1)} %make_hidden.5.refs_0_), channel_id=1, source_target_pairs={{1,0},{0,1},{3,2},{2,3},{5,4},{4,5},{7,6},{6,7},{9,8},{8,9},{11,10... | collective-permute-start | bytes 786440 | tf_op jit(solution)/shard_map/ppermute | solution.py:606
  85.9 5.5 %collective-permute-start.13 = (bf16[64,2048]{1,0:T(8,128)(2,1)S(1)}, bf16[64,2048]{1,0:T(8,128)(2,1)S(1)}, u32[]{:S(2)}, u32[]{:S(2)}) collective-permute-start(bf16[64,2048]{1,0:T(8,128)(2,1)S(1)} %get-tuple-element.55), channel_id=1, source_target_pairs={{0,2},{2,0},{4,6},{6,4},{8,10},{10,8},{12,14},{14,12},{16,18},{18,... | collective-permute-start | bytes 786440 | tf_op jit(solution)/shard_map/ppermute | solution.py:569
  89.7 2.4 %collective-permute-start.33 = (bf16[128,2048]{1,0:T(8,128)(2,1)S(1)}, bf16[128,2048]{1,0:T(8,128)(2,1)S(1)}, u32[]{:S(2)}, u32[]{:S(2)}) collective-permute-start(bf16[128,2048]{1,0:T(8,128)(2,1)S(1)} %get-tuple-element.65), channel_id=1, source_target_pairs={{0,2},{2,0},{4,6},{6,4},{8,10},{10,8},{12,14},{14,12},{16,18},{18,... | collective-permute-start | bytes 1572872 | tf_op jit(solution)/shard_map/ppermute | solution.py:569
  89.9 21.1 %collective-permute-start.22 = (bf16[32,2048]{1,0:T(8,128)(2,1)S(1)}, bf16[32,2048]{1,0:T(8,128)(2,1)S(1)}, u32[]{:S(2)}, u32[]{:S(2)}) collective-permute-start(bf16[32,2048]{1,0:T(8,128)(2,1)S(1)} %slice.64), channel_id=1, source_target_pairs={{0,4},{2,6},{4,0},{6,2},{8,12},{10,14},{12,8},{14,10},{16,20},{18,... | collective-permute-start | bytes 393224 | tf_op jit(solution)/shard_map/ppermute | solution.py:569
  91.5 7.6 %collective-permute-start.14 = (bf16[32,2048]{1,0:T(8,128)(2,1)S(1)}, bf16[32,2048]{1,0:T(8,128)(2,1)S(1)}, u32[]{:S(2)}, u32[]{:S(2)}) collective-permute-start(bf16[32,2048]{1,0:T(8,128)(2,1)S(1)} %slice.65), channel_id=1, source_target_pairs={{0,4},{2,6},{4,0},{6,2},{8,12},{10,14},{12,8},{14,10},{16,20},{18,... | collective-permute-start | bytes 393224 | tf_op jit(solution)/shard_map/ppermute | solution.py:569
  92.3 12.0 %collective-permute-start.34 = (bf16[64,2048]{1,0:T(8,128)(2,1)S(1)}, bf16[64,2048]{1,0:T(8,128)(2,1)S(1)}, u32[]{:S(2)}, u32[]{:S(2)}) collective-permute-start(bf16[64,2048]{1,0:T(8,128)(2,1)S(1)} %slice.63), channel_id=1, source_target_pairs={{0,4},{2,6},{4,0},{6,2},{8,12},{10,14},{12,8},{14,10},{16,20},{18,... | collective-permute-start | bytes 786440 | tf_op jit(solution)/shard_map/ppermute | solution.py:569
  99.2 11.8 %collective-permute-start.15 = (bf16[32,2048]{1,0:T(8,128)(2,1)S(1)}, bf16[32,2048]{1,0:T(8,128)(2,1)S(1)}, u32[]{:S(2)}, u32[]{:S(2)}) collective-permute-start(bf16[32,2048]{1,0:T(8,128)(2,1)S(1)} %fusion.5), channel_id=1, source_target_pairs={{0,8},{2,10},{4,12},{6,14},{8,0},{10,2},{12,4},{14,6},{16,24},{18,... | collective-permute-start | bytes 393224 | tf_op jit(solution)/shard_map/ppermute | solution.py:569
  104.4 8.3 %collective-permute-start.36 = (bf16[32,2048]{1,0:T(8,128)(2,1)S(1)}, bf16[32,2048]{1,0:T(8,128)(2,1)S(1)}, u32[]{:S(2)}, u32[]{:S(2)}) collective-permute-start(bf16[32,2048]{1,0:T(8,128)(2,1)S(1)} %get-tuple-element.69), channel_id=1, source_target_pairs={{0,24},{2,26},{4,28},{6,30},{8,16},{10,18},{12,20},{14,22},{16,8},... | collective-permute-start | bytes 393224 | tf_op jit(solution)/shard_map/ppermute | solution.py:569
  106.8 11.3 %collective-permute-start.35 = (bf16[32,2048]{1,0:T(8,128)(2,1)S(1)}, bf16[32,2048]{1,0:T(8,128)(2,1)S(1)}, u32[]{:S(2)}, u32[]{:S(2)}) collective-permute-start(bf16[32,2048]{1,0:T(8,128)(2,1)S(1)} %get-tuple-element.68), channel_id=1, source_target_pairs={{0,16},{2,18},{4,20},{6,22},{8,24},{10,26},{12,28},{14,30},{16,0},... | collective-permute-start | bytes 393224 | tf_op jit(solution)/shard_map/ppermute | solution.py:569
